TPU v7x, 512 devices: a whole 4x8x8 slice. The times are simulated.
512 devices in a mesh: half: 2 (over x_lo), gx: 16 (over y, core), gy: 16 (over z, x_hi).
Axes of the slice: x: 4 (x_hi: 2, x_lo: 2; x = x_hi * 2 + x_lo), y: 8, z: 8, core: 2. Of those that a mesh axis runs over, the one named last changes fastest.
Arguments:
- current: float32 [2, 128, 73728], P('half', 'gx', 'gy'), may hold values from -6 to 6
- previous: float32 [2, 128, 73728], P('half', 'gx', 'gy'), may hold values from -6 to 6
- material: float32 [2, 128, 73728], P('half', 'gx', 'gy'), may hold values from 0.4 to 1.6
- prior: float32 [4, 128, 512], P(None, 'gx', 'gy'), may hold values from -6 to 6
Outputs:
- fields: float32 [2, 128, 73728], P('half', 'gx', 'gy')
- seafloor: float32 [2, 4, 128, 512], P('half', None, 'gx', 'gy')
All inputs are finite; a program needn't handle non-finite values.
Results may differ from a plain program's by a relative error of at most 0.00002.
Values sent between devices are 32-bit elements; how exact they have to be, the bound alone decides.
A program may use at most 64 MiB of HBM per device.

v0:
```python
import jax
import jax.numpy as jnp
from jax import lax
from jax.sharding import PartitionSpec as P

STEPS = 4
PLANES = 144


TIME_STEP = 0.22
RELAXATION = 0.5


def with_halo(cells, sides, width):
    for axis, dim in sides:
        count = lax.axis_size(axis)
        ends = count - 1
        head = lax.slice_in_dim(cells, 0, width, axis=dim)
        tail = lax.slice_in_dim(cells, cells.shape[dim] - width, cells.shape[dim], axis=dim)
        cells = jnp.concatenate(
            [
                lax.ppermute(tail, axis, [(i, (i + 1) % count) for i in range(ends)]),
                cells,
                lax.ppermute(head, axis, [((i + 1) % count, i) for i in range(ends)]),
            ],
            axis=dim,
        )
    return cells


def shifted(shard, axis, by):
    peers = lax.axis_size(axis)
    pairs = [(i, i + by) for i in range(peers) if 0 <= i + by < peers]
    return lax.ppermute(shard, axis, pairs)


def from_above(field):
    return jnp.concatenate([jnp.zeros_like(field[:, :, :1]), field[:, :, :-1]], axis=2)


def from_below(field):
    return jnp.concatenate([field[:, :, 1:], jnp.zeros_like(field[:, :, :1])], axis=2)


def water_update(padded, field_now, field_old, moduli, ghost_row):
    lateral = padded[2:, 1:-1] + padded[:-2, 1:-1] + padded[1:-1, 2:] + padded[1:-1, :-2]
    cell_above = from_above(field_now)
    cell_below = jnp.concatenate(
        [field_now[:, :, 1:], field_now[:, :, -1:] - ghost_row[:, :, None]], axis=2
    )
    laplace = lateral + cell_above + cell_below - 6.0 * field_now
    return 2.0 * field_now - field_old + TIME_STEP * TIME_STEP * moduli * laplace


def seabed_update(padded, field_now, field_old, moduli, load_row):
    depth = field_now.shape[2]
    thick = depth // 3
    planes = lax.broadcasted_iota(jnp.int32, (1, 1, depth), 2)
    level_in = planes % thick
    not_top = (level_in != 0).astype(jnp.float32)
    not_bottom = (level_in != thick - 1).astype(jnp.float32)
    top_vertical = (planes == 2 * thick).astype(jnp.float32)
    curve_xx = padded[2:, 1:-1] - 2.0 * field_now + padded[:-2, 1:-1]
    curve_yy = padded[1:-1, 2:] - 2.0 * field_now + padded[1:-1, :-2]
    curve_zz = (
        from_below(field_now) * not_bottom - 2.0 * field_now + from_above(field_now) * not_top
    )
    cross_xy = (padded[2:, 2:] - padded[2:, :-2] - padded[:-2, 2:] + padded[:-2, :-2]) * 0.25
    slope_x = padded[2:, 1:-1] - padded[:-2, 1:-1]
    slope_y = padded[1:-1, 2:] - padded[1:-1, :-2]
    cross_xz = (from_below(slope_x) * not_bottom - from_above(slope_x) * not_top) * 0.25
    cross_yz = (from_below(slope_y) * not_bottom - from_above(slope_y) * not_top) * 0.25

    def component(field, which):
        return field[:, :, which * thick : (which + 1) * thick]

    grad_div = jnp.concatenate(
        [
            component(curve_xx, 0) + component(cross_xy, 1) + component(cross_xz, 2),
            component(cross_xy, 0) + component(curve_yy, 1) + component(cross_yz, 2),
            component(cross_xz, 0) + component(cross_yz, 1) + component(curve_zz, 2),
        ],
        axis=2,
    )
    laplace = curve_xx + curve_yy + curve_zz
    bulk_term = jnp.concatenate([component(moduli, 0)] * 3, axis=2)
    shear_term = jnp.concatenate([component(moduli, 1)] * 3, axis=2)
    buoyant = jnp.concatenate([component(moduli, 2)] * 3, axis=2)
    acceleration = buoyant * (
        bulk_term * grad_div + shear_term * laplace + top_vertical * load_row[:, :, None]
    )
    updated = 2.0 * field_now - field_old + TIME_STEP * TIME_STEP * acceleration
    return (updated, acceleration[:, :, 2 * thick])


def advance(is_fluid, field_now, field_old, moduli, ghost_row, load_row, inside):
    padded = jnp.pad(field_now, ((1, 1), (1, 1), (0, 0)))
    blank = jnp.zeros(field_now.shape[:2], jnp.float32)

    def water_branch():
        return (water_update(padded, field_now, field_old, moduli, ghost_row), field_now, blank)

    def seabed_branch():
        updated, motion_row = seabed_update(padded, field_now, field_old, moduli, load_row)
        return (updated, field_now, motion_row)

    updated, older, motion_row = lax.cond(is_fluid, water_branch, seabed_branch)
    updated = updated * inside
    return (updated, older, motion_row)


def crop_cells(field, margin):
    return field[margin : field.shape[0] - margin, margin : field.shape[1] - margin]


def crop_waves(waves, margin):
    return waves[:, margin : waves.shape[1] - margin, margin : waves.shape[2] - margin]


def on_device(current, previous, material, prior):
    block_x = current.shape[1]
    block_y = current.shape[2] // PLANES
    cube = (block_x, block_y, PLANES)
    field_now = current[0].reshape(cube)
    field_old = previous[0].reshape(cube)
    moduli = material[0].reshape(cube)
    is_fluid = lax.axis_index("half") == 0
    inside = None
    margin = 0
    margin = STEPS
    stacked = jnp.stack([field_now, field_old, moduli])
    widened = with_halo(stacked, (("gx", 1), ("gy", 2)), STEPS)
    field_now, field_old, moduli = (widened[0], widened[1], widened[2])
    forcing = with_halo(prior, (("gx", 1), ("gy", 2)), STEPS)
    span_x = block_x + 2 * STEPS
    span_y = block_y + 2 * STEPS
    global_x = (
        lax.broadcasted_iota(jnp.int32, (span_x, 1, 1), 0) + lax.axis_index("gx") * block_x - STEPS
    )
    global_y = (
        lax.broadcasted_iota(jnp.int32, (1, span_y, 1), 1) + lax.axis_index("gy") * block_y - STEPS
    )
    inside_x = (global_x >= 0) & (global_x < block_x * lax.axis_size("gx"))
    inside_y = (global_y >= 0) & (global_y < block_y * lax.axis_size("gy"))
    inside = (inside_x & inside_y).astype(jnp.float32)
    motions = []
    arrived = []
    for instant in range(STEPS):
        sample_row = shifted(field_now[:, :, -1], "half", 1)
        arrived.append(sample_row)
        field_now, field_old, motion_row = advance(
            is_fluid, field_now, field_old, moduli, forcing[instant], sample_row, inside
        )
        motions.append(motion_row)
    received = jnp.stack(arrived)
    returned = shifted(crop_waves(jnp.stack(motions), margin), "half", -1)
    relaxed = RELAXATION * returned + (1.0 - RELAXATION) * prior
    waveform = jnp.where(is_fluid, relaxed, crop_waves(received, margin))
    merged = crop_cells(field_now, margin).reshape((1, block_x, block_y * PLANES))
    return (merged, waveform[None])


def solution(mesh):
    placed = (
        P("half", "gx", "gy"),
        P("half", "gx", "gy"),
        P("half", "gx", "gy"),
        P(None, "gx", "gy"),
    )
    return jax.shard_map(
        on_device,
        mesh=mesh,
        in_specs=placed,
        out_specs=(P("half", "gx", "gy"), P("half", None, "gx", "gy")),
        check_vma=False,
    )
```

profile of v0, /device:TPU:288, one launch (start us, length us, event | category | flops | bytes accessed | tf_op | source)
XLA Modules:
  0.0 130.6 jit_solution(2062032956471737226)
XLA Ops:
  3.2 1.9 %collective-permute-start = (f32[3,4,32,144]{3,2,1,0:T(8,128)S(1)}, f32[3,4,32,144]{3,2,1,0:T(8,128)S(1)}, u32[]{:S(2)}, u32[]{:S(2)}) collective-permute-start(f32[3,4,32,144]{3,2,1,0:T(8,128)S(1)} %get-tuple-element.415), channel_id=1, source_target_pairs={{0,16},{16,32},{32,48},{48,64},{64,80},{80,96},{96,112},{112,128},... | collective-permute-start | bytes 663560 | tf_op jit(solution)/shard_map/ppermute | solution.py:22
  5.2 4.9 %collective-permute-start.1 = (f32[3,4,32,144]{3,2,1,0:T(8,128)S(1)}, f32[3,4,32,144]{3,2,1,0:T(8,128)S(1)}, u32[]{:S(2)}, u32[]{:S(2)}) collective-permute-start(f32[3,4,32,144]{3,2,1,0:T(8,128)S(1)} %get-tuple-element.416), channel_id=1, source_target_pairs={{16,0},{32,16},{48,32},{64,48},{80,64},{96,80},{112,96},{128,112},... | collective-permute-start | bytes 663560 | tf_op jit(solution)/shard_map/ppermute | solution.py:24
  10.0 1.9 %collective-permute-start.5 = (f32[4,4,32]{2,1,0:T(4,128)S(1)}, f32[4,4,32]{2,1,0:T(4,128)S(1)}, u32[]{:S(2)}, u32[]{:S(2)}) collective-permute-start(f32[4,4,32]{2,1,0:T(4,128)S(1)} %get-tuple-element.419), channel_id=1, source_target_pairs={{0,16},{16,32},{32,48},{48,64},{64,80},{80,96},{96,112},{112,128},... | collective-permute-start | bytes 6152 | tf_op jit(solution)/shard_map/ppermute | solution.py:22
  12.0 4.9 %collective-permute-start.6 = (f32[4,4,32]{2,1,0:T(4,128)S(1)}, f32[4,4,32]{2,1,0:T(4,128)S(1)}, u32[]{:S(2)}, u32[]{:S(2)}) collective-permute-start(f32[4,4,32]{2,1,0:T(4,128)S(1)} %get-tuple-element.420), channel_id=1, source_target_pairs={{16,0},{32,16},{48,32},{64,48},{80,64},{96,80},{112,96},{128,112},... | collective-permute-start | bytes 6152 | tf_op jit(solution)/shard_map/ppermute | solution.py:24
  18.3 4.9 %collective-permute-start.2 = (f32[3,16,4,144]{3,2,1,0:T(4,128)S(1)}, f32[3,16,4,144]{3,2,1,0:T(4,128)S(1)}, u32[]{:S(2)}, u32[]{:S(2)}) collective-permute-start(f32[3,16,4,144]{3,2,1,0:T(4,128)S(1)} %get-tuple-element.413), channel_id=1, source_target_pairs={{0,1},{1,2},{2,3},{3,4},{4,5},{5,6},{6,7},{7,8},{8,9},{9,10},{10,1... | collective-permute-start | bytes 331784 | tf_op jit(solution)/shard_map/ppermute | solution.py:22
  23.2 4.5 %collective-permute-start.3 = (f32[3,16,4,144]{3,2,1,0:T(4,128)S(1)}, f32[3,16,4,144]{3,2,1,0:T(4,128)S(1)}, u32[]{:S(2)}, u32[]{:S(2)}) collective-permute-start(f32[3,16,4,144]{3,2,1,0:T(4,128)S(1)} %get-tuple-element.414), channel_id=1, source_target_pairs={{1,0},{2,1},{3,2},{4,3},{5,4},{6,5},{7,6},{8,7},{9,8},{10,9},{11,1... | collective-permute-start | bytes 331784 | tf_op jit(solution)/shard_map/ppermute | solution.py:24
  27.9 2.8 %collective-permute-start.7 = (f32[4,16,4]{2,1,0:T(8,128)S(1)}, f32[4,16,4]{2,1,0:T(8,128)S(1)}, u32[]{:S(2)}, u32[]{:S(2)}) collective-permute-start(f32[4,16,4]{2,1,0:T(8,128)S(1)} %get-tuple-element.417), channel_id=1, source_target_pairs={{0,1},{1,2},{2,3},{3,4},{4,5},{5,6},{6,7},{7,8},{8,9},{9,10},{10,1... | collective-permute-start | bytes 3080 | tf_op jit(solution)/shard_map/ppermute | solution.py:22
  30.7 6.6 %collective-permute-start.8 = (f32[4,16,4]{2,1,0:T(8,128)S(1)}, f32[4,16,4]{2,1,0:T(8,128)S(1)}, u32[]{:S(2)}, u32[]{:S(2)}) collective-permute-start(f32[4,16,4]{2,1,0:T(8,128)S(1)} %get-tuple-element.418), channel_id=1, source_target_pairs={{1,0},{2,1},{3,2},{4,3},{5,4},{6,5},{7,6},{8,7},{9,8},{10,9},{11,1... | collective-permute-start | bytes 3080 | tf_op jit(solution)/shard_map/ppermute | solution.py:24
  40.3 4.0 %collective-permute-start.4 = (f32[16,40]{1,0:T(8,128)S(1)}, f32[16,40]{1,0:T(8,128)}, u32[]{:S(2)}, u32[]{:S(2)}) collective-permute-start(f32[16,40]{1,0:T(8,128)S(1)} %slice_reduce_fusion), channel_id=1, source_target_pairs={{0,256},{1,257},{2,258},{3,259},{4,260},{5,261},{6,262},{7,263},{8... | collective-permute-start | bytes 7688 | tf_op jit(solution)/shard_map/ppermute | solution.py:34
  45.0 2.1 %pad.41 = f32[18,42,144]{2,1,0:T(8,128)} pad(f32[16,40,144]{2,1,0:T(8,128)} %get-tuple-element.412, f32[]{:T(128)} %constant.152.clone.1), padding=1_1x1_1x0_0 | pad | bytes 804100 | tf_op jit(solution)/shard_map/jit(_pad)/pad | solution.py:97
  47.1 14.6 %conditional.4 = (f32[1,16,40]{2,1,0:T(8,128)S(1)}, f32[16,40,144]{1,0,2:T(8,128)S(1)}) conditional(s32[]{:T(128)} %convert_element_type.147, (f32[16,40,144]{2,1,0:T(8,128)}, f32[16,40,144]{2,1,0:T(8,128)}, f32[16,40,144]{2,1,0:T(8,128)}, f32[18,42,144]{2,1,0:T(8,128)}, f32[16,40]{1,0:T(8,128)}) %tuple.48, (f32[16,40,144]{2,1,0:T(8,128)}, ...), branch_computations={%region_0.1_spmd, %region_1.2_spmd} | conditional | flops 4149792 | bytes 28853916 | solution.py:107
  47.1 1.7 %copy.263 = f32[16,40,144]{1,0,2:T(8,128)S(1)} copy(f32[16,40,144]{2,1,0:T(8,128)} %get-tuple-element.261) | data formatting | bytes 737280 | tf_op jit(solution)/shard_map
  48.8 1.6 %fusion.25 = (f32[16,40,143]{1,0,2:T(8,128)}, f32[16,40,143]{1,0,2:T(8,128)}) fusion(f32[16,40,144]{1,0,2:T(8,128)S(1)} %copy.263), kind=kLoop, calls=%fused_computation.158 | loop fusion | bytes 1464320 | tf_op jit(solution)/shard_map/cond/branch_1_fun/slice | solution.py:38
  51.2 1.9 %copy.266 = f32[18,42,144]{1,0,2:T(8,128)S(1)} copy(f32[18,42,144]{2,1,0:T(8,128)} %get-tuple-element.264) | data formatting | bytes 870912 | tf_op jit(solution)/shard_map
  53.1 2.6 %copy.264 = f32[16,40,144]{1,0,2:T(8,128)} copy(f32[16,40,144]{2,1,0:T(8,128)} %get-tuple-element.262) | data formatting | bytes 737280 | tf_op jit(solution)/shard_map
  55.7 2.6 %copy.265 = f32[16,40,144]{1,0,2:T(8,128)} copy(f32[16,40,144]{2,1,0:T(8,128)} %get-tuple-element.263) | data formatting | bytes 737280 | tf_op jit(solution)/shard_map
  58.3 3.3 %fusion.7 = f32[16,40,144]{1,0,2:T(8,128)S(1)} fusion(f32[18,42,144]{1,0,2:T(8,128)S(1)} %copy.266, f32[16,40,1]{1,0,2:T(8,128)S(1)} %slice_subtract_fusion.4, f32[16,40,143]{1,0,2:T(8,128)} %get-tuple-element.309, f32[16,40,144]{1,0,2:T(8,128)S(1)} %copy.263, f32[16,40,143]{1,0,2:T(8,128)} %get-tuple-element.308, f32[16,40,144]{1,0,2:T(8,128)} %copy.265, ...), kind=kLoop, calls=%fused_computation.33 | loop fusion | flops 1198080 | bytes 3683840 | tf_op jit(solution)/shard_map/cond/branch_1_fun/add | solution.py:52
  62.5 9.1 %collective-permute-start.9 = (f32[16,40]{1,0:T(8,128)S(1)}, f32[16,40]{1,0:T(8,128)}, u32[]{:S(2)}, u32[]{:S(2)}) collective-permute-start(f32[16,40]{1,0:T(8,128)S(1)} %slice_bitcast_fusion.9), channel_id=1, source_target_pairs={{0,256},{1,257},{2,258},{3,259},{4,260},{5,261},{6,262},{7,263},{8... | collective-permute-start | bytes 7688 | tf_op jit(solution)/shard_map/ppermute | solution.py:34
  72.4 10.9 %conditional.5 = (f32[1,16,40]{2,1,0:T(8,128)S(1)}, f32[16,40,144]{1,0,2:T(8,128)S(1)}) conditional(s32[]{:T(128)} %convert_element_type.147, (f32[16,40,144]{1,0,2:T(8,128)S(1)}, f32[16,40,144]{2,1,0:T(8,128)}, f32[16,40,144]{2,1,0:T(8,128)}, f32[18,42,144]{1,0,2:T(8,128)S(1)}, f32[16,40]{1,0:T(8,128)}) %tuple.50, (f32[16,40,144]{1,0,2:T(8,128)S(1)}, ...), branch_computations={%region_2.3_spmd, %region_3.4_spmd} | conditional | flops 4149792 | bytes 27245724 | solution.py:107
  74.7 2.6 %copy.270 = f32[16,40,144]{1,0,2:T(8,128)} copy(f32[16,40,144]{2,1,0:T(8,128)} %get-tuple-element.272) | data formatting | bytes 737280 | tf_op jit(solution)/shard_map
  77.3 2.6 %copy.271 = f32[16,40,144]{1,0,2:T(8,128)} copy(f32[16,40,144]{2,1,0:T(8,128)} %get-tuple-element.273) | data formatting | bytes 737280 | tf_op jit(solution)/shard_map
  80.0 3.3 %fusion.12 = f32[16,40,144]{1,0,2:T(8,128)S(1)} fusion(f32[16,40,1]{1,0,2:T(8,128)S(1)} %bitcast_subtract_fusion, f32[16,40,143]{1,0,2:T(8,128)} %get-tuple-element.311, f32[16,40,144]{1,0,2:T(8,128)S(1)} %get-tuple-element.103, f32[16,40,143]{1,0,2:T(8,128)} %get-tuple-element.310, f32[18,42,144]{1,0,2:T(8,128)S(1)} %get-tuple-element.106, ...), kind=kLoop, calls=%fused_computation.65 | loop fusion | flops 1198080 | bytes 3683840 | tf_op jit(solution)/shard_map/cond/branch_1_fun/add | solution.py:52
  84.1 8.6 %collective-permute-start.10 = (f32[16,40]{1,0:T(8,128)S(1)}, f32[16,40]{1,0:T(8,128)}, u32[]{:S(2)}, u32[]{:S(2)}) collective-permute-start(f32[16,40]{1,0:T(8,128)S(1)} %slice_bitcast_fusion.8), channel_id=1, source_target_pairs={{0,256},{1,257},{2,258},{3,259},{4,260},{5,261},{6,262},{7,263},{8... | collective-permute-start | bytes 7688 | tf_op jit(solution)/shard_map/ppermute | solution.py:34
  93.4 8.3 %conditional.6 = (f32[1,16,40]{2,1,0:T(8,128)S(1)}, f32[16,40,144]{1,0,2:T(8,128)S(1)}) conditional(s32[]{:T(128)} %convert_element_type.147, (f32[16,40,144]{1,0,2:T(8,128)S(1)}, f32[16,40,144]{1,0,2:T(8,128)}, f32[16,40,144]{2,1,0:T(8,128)}, f32[18,42,144]{1,0,2:T(8,128)S(1)}, f32[16,40]{1,0:T(8,128)}) %tuple.192, (f32[16,40,144]{1,0,2:T(8,128)S(1)}, ...), branch_computations={%region_4.5_spmd, %region_5.6_spmd} | conditional | flops 4149792 | bytes 27983032 | solution.py:107
  95.7 2.6 %copy.276 = f32[16,40,144]{1,0,2:T(8,128)} copy(f32[16,40,144]{2,1,0:T(8,128)} %get-tuple-element.283) | data formatting | bytes 737280 | tf_op jit(solution)/shard_map
  98.4 3.3 %fusion.17 = f32[16,40,144]{1,0,2:T(8,128)S(1)} fusion(f32[16,40,1]{1,0,2:T(8,128)S(1)} %bitcast_subtract_fusion.1, f32[16,40,143]{1,0,2:T(8,128)} %get-tuple-element.313, f32[16,40,144]{1,0,2:T(8,128)S(1)} %get-tuple-element.113, f32[16,40,143]{1,0,2:T(8,128)} %get-tuple-element.312, f32[18,42,144]{1,0,2:T(8,128)S(1)} %get-tuple-element.116, ...), kind=kLoop, calls=%fused_computation.95 | loop fusion | flops 1198080 | bytes 3683840 | tf_op jit(solution)/shard_map/cond/branch_1_fun/add | solution.py:52
  102.6 7.7 %collective-permute-start.11 = (f32[16,40]{1,0:T(8,128)S(1)}, f32[16,40]{1,0:T(8,128)}, u32[]{:S(2)}, u32[]{:S(2)}) collective-permute-start(f32[16,40]{1,0:T(8,128)S(1)} %slice_bitcast_fusion.7), channel_id=1, source_target_pairs={{0,256},{1,257},{2,258},{3,259},{4,260},{5,261},{6,262},{7,263},{8... | collective-permute-start | bytes 7688 | tf_op jit(solution)/shard_map/ppermute | solution.py:34
  111.5 8.5 %conditional.7 = (f32[1,16,40]{2,1,0:T(8,128)S(1)}, f32[16,40,144]{1,0,2:T(8,128)S(1)}) conditional(s32[]{:T(128)} %convert_element_type.147, (f32[16,40,144]{1,0,2:T(8,128)S(1)}, f32[16,40,144]{1,0,2:T(8,128)S(1)}, f32[16,40,144]{2,1,0:T(8,128)}, f32[18,42,144]{1,0,2:T(8,128)S(1)}, f32[16,40]{1,0:T(8,128)}) %tuple.54, (f32[16,40,144]{1,0,2:T(8,128)S(1)}, ...), branch_computations={%region_6.7_spmd, %region_7.8_spmd} | conditional | flops 4149792 | bytes 29457620 | solution.py:107
  111.5 1.7 %fusion.28 = (f32[16,40,143]{1,0,2:T(8,128)}, f32[16,40,143]{1,0,2:T(8,128)}) fusion(f32[16,40,144]{1,0,2:T(8,128)S(1)} %get-tuple-element.123), kind=kLoop, calls=%fused_computation.161 | loop fusion | bytes 1464320 | tf_op jit(solution)/shard_map/cond/branch_1_fun/slice | solution.py:38
  114.0 2.6 %copy.281 = f32[16,40,144]{1,0,2:T(8,128)} copy(f32[16,40,144]{2,1,0:T(8,128)} %get-tuple-element.293) | data formatting | bytes 737280 | tf_op jit(solution)/shard_map
  116.6 3.3 %fusion.22 = f32[16,40,144]{1,0,2:T(8,128)S(1)} fusion(f32[16,40,1]{1,0,2:T(8,128)S(1)} %bitcast_subtract_fusion.2, f32[16,40,143]{1,0,2:T(8,128)} %get-tuple-element.315, f32[16,40,144]{1,0,2:T(8,128)} %copy-done.4, f32[16,40,143]{1,0,2:T(8,128)} %get-tuple-element.314, f32[18,42,144]{1,0,2:T(8,128)S(1)} %get-tuple-element.126, f32[16,40,144]{1,0,2:T(8,128)} %copy.281, ...), kind=kLoop, calls=%fused_computation.125 | loop fusion | flops 1198080 | bytes 3683840 | tf_op jit(solution)/shard_map/cond/branch_1_fun/add | solution.py:52
  124.1 5.0 %collective-permute-done.12 = f32[4,8,32]{2,1,0:T(8,128)S(1)} collective-permute-done((f32[4,8,32]{2,1,0:T(8,128)S(1)}, f32[4,8,32]{2,1,0:T(8,128)S(1)}, u32[]{:S(2)}, u32[]{:S(2)}) %collective-permute-start.12) | collective-permute-done | bytes 4128 | tf_op jit(solution)/shard_map/ppermute | solution.py:34
  (72 shorter events, 24.5 us)
Async XLA Ops:
  0.6 2.3 %copy-start.27 = (f32[1,8,4608]{2,1,0:T(8,128)S(1)}, f32[1,8,4608]{2,1,0:T(8,128)}, u32[]{:S(2)}) copy-start(f32[1,8,4608]{2,1,0:T(8,128)} %param.14) | copy-start | bytes 442372
  3.1 6.9 %copy-start.25 = (f32[4,8,32]{2,1,0:T(8,128)S(1)}, f32[4,8,32]{2,1,0:T(8,128)}, u32[]{:S(2)}) copy-start(f32[4,8,32]{2,1,0:T(8,128)} %param.15) | copy-start | bytes 12292
  3.2 15.0 %collective-permute-start = (f32[3,4,32,144]{3,2,1,0:T(8,128)S(1)}, f32[3,4,32,144]{3,2,1,0:T(8,128)S(1)}, u32[]{:S(2)}, u32[]{:S(2)}) collective-permute-start(f32[3,4,32,144]{3,2,1,0:T(8,128)S(1)} %get-tuple-element.415), channel_id=1, source_target_pairs={{0,16},{16,32},{32,48},{48,64},{64,80},{80,96},{96,112},{112,128},... | collective-permute-start | bytes 663560 | tf_op jit(solution)/shard_map/ppermute | solution.py:22
  5.2 13.0 %collective-permute-start.1 = (f32[3,4,32,144]{3,2,1,0:T(8,128)S(1)}, f32[3,4,32,144]{3,2,1,0:T(8,128)S(1)}, u32[]{:S(2)}, u32[]{:S(2)}) collective-permute-start(f32[3,4,32,144]{3,2,1,0:T(8,128)S(1)} %get-tuple-element.416), channel_id=1, source_target_pairs={{16,0},{32,16},{48,32},{64,48},{80,64},{96,80},{112,96},{128,112},... | collective-permute-start | bytes 663560 | tf_op jit(solution)/shard_map/ppermute | solution.py:24
  10.0 7.5 %collective-permute-start.5 = (f32[4,4,32]{2,1,0:T(4,128)S(1)}, f32[4,4,32]{2,1,0:T(4,128)S(1)}, u32[]{:S(2)}, u32[]{:S(2)}) collective-permute-start(f32[4,4,32]{2,1,0:T(4,128)S(1)} %get-tuple-element.419), channel_id=1, source_target_pairs={{0,16},{16,32},{32,48},{48,64},{64,80},{80,96},{96,112},{112,128},... | collective-permute-start | bytes 6152 | tf_op jit(solution)/shard_map/ppermute | solution.py:22
  12.0 6.2 %collective-permute-start.6 = (f32[4,4,32]{2,1,0:T(4,128)S(1)}, f32[4,4,32]{2,1,0:T(4,128)S(1)}, u32[]{:S(2)}, u32[]{:S(2)}) collective-permute-start(f32[4,4,32]{2,1,0:T(4,128)S(1)} %get-tuple-element.420), channel_id=1, source_target_pairs={{16,0},{32,16},{48,32},{64,48},{80,64},{96,80},{112,96},{128,112},... | collective-permute-start | bytes 6152 | tf_op jit(solution)/shard_map/ppermute | solution.py:24
  18.3 19.0 %collective-permute-start.2 = (f32[3,16,4,144]{3,2,1,0:T(4,128)S(1)}, f32[3,16,4,144]{3,2,1,0:T(4,128)S(1)}, u32[]{:S(2)}, u32[]{:S(2)}) collective-permute-start(f32[3,16,4,144]{3,2,1,0:T(4,128)S(1)} %get-tuple-element.413), channel_id=1, source_target_pairs={{0,1},{1,2},{2,3},{3,4},{4,5},{5,6},{6,7},{7,8},{8,9},{9,10},{10,1... | collective-permute-start | bytes 331784 | tf_op jit(solution)/shard_map/ppermute | solution.py:22
  23.2 14.1 %collective-permute-start.3 = (f32[3,16,4,144]{3,2,1,0:T(4,128)S(1)}, f32[3,16,4,144]{3,2,1,0:T(4,128)S(1)}, u32[]{:S(2)}, u32[]{:S(2)}) collective-permute-start(f32[3,16,4,144]{3,2,1,0:T(4,128)S(1)} %get-tuple-element.414), channel_id=1, source_target_pairs={{1,0},{2,1},{3,2},{4,3},{5,4},{6,5},{7,6},{8,7},{9,8},{10,9},{11,1... | collective-permute-start | bytes 331784 | tf_op jit(solution)/shard_map/ppermute | solution.py:24
  27.9 16.4 %collective-permute-start.7 = (f32[4,16,4]{2,1,0:T(8,128)S(1)}, f32[4,16,4]{2,1,0:T(8,128)S(1)}, u32[]{:S(2)}, u32[]{:S(2)}) collective-permute-start(f32[4,16,4]{2,1,0:T(8,128)S(1)} %get-tuple-element.417), channel_id=1, source_target_pairs={{0,1},{1,2},{2,3},{3,4},{4,5},{5,6},{6,7},{7,8},{8,9},{9,10},{10,1... | collective-permute-start | bytes 3080 | tf_op jit(solution)/shard_map/ppermute | solution.py:22
  30.7 13.6 %collective-permute-start.8 = (f32[4,16,4]{2,1,0:T(8,128)S(1)}, f32[4,16,4]{2,1,0:T(8,128)S(1)}, u32[]{:S(2)}, u32[]{:S(2)}) collective-permute-start(f32[4,16,4]{2,1,0:T(8,128)S(1)} %get-tuple-element.418), channel_id=1, source_target_pairs={{1,0},{2,1},{3,2},{4,3},{5,4},{6,5},{7,6},{8,7},{9,8},{10,9},{11,1... | collective-permute-start | bytes 3080 | tf_op jit(solution)/shard_map/ppermute | solution.py:24
  40.3 6.8 %collective-permute-start.4 = (f32[16,40]{1,0:T(8,128)S(1)}, f32[16,40]{1,0:T(8,128)}, u32[]{:S(2)}, u32[]{:S(2)}) collective-permute-start(f32[16,40]{1,0:T(8,128)S(1)} %slice_reduce_fusion), channel_id=1, source_target_pairs={{0,256},{1,257},{2,258},{3,259},{4,260},{5,261},{6,262},{7,263},{8... | collective-permute-start | bytes 7688 | tf_op jit(solution)/shard_map/ppermute | solution.py:34
  61.7 0.8 copy-start.28
  62.5 9.9 %copy-start = (f32[16,40,144]{1,0,2:T(8,128)}, f32[16,40,144]{1,0,2:T(8,128)S(1)}, u32[]{:S(2)}) copy-start(f32[16,40,144]{1,0,2:T(8,128)S(1)} %broadcast_multiply_fusion.2) | copy-start | bytes 1105924
  62.5 9.9 %collective-permute-start.9 = (f32[16,40]{1,0:T(8,128)S(1)}, f32[16,40]{1,0:T(8,128)}, u32[]{:S(2)}, u32[]{:S(2)}) collective-permute-start(f32[16,40]{1,0:T(8,128)S(1)} %slice_bitcast_fusion.9), channel_id=1, source_target_pairs={{0,256},{1,257},{2,258},{3,259},{4,260},{5,261},{6,262},{7,263},{8... | collective-permute-start | bytes 7688 | tf_op jit(solution)/shard_map/ppermute | solution.py:34
  83.3 0.8 copy-start.29
  84.1 9.3 %collective-permute-start.10 = (f32[16,40]{1,0:T(8,128)S(1)}, f32[16,40]{1,0:T(8,128)}, u32[]{:S(2)}, u32[]{:S(2)}) collective-permute-start(f32[16,40]{1,0:T(8,128)S(1)} %slice_bitcast_fusion.8), channel_id=1, source_target_pairs={{0,256},{1,257},{2,258},{3,259},{4,260},{5,261},{6,262},{7,263},{8... | collective-permute-start | bytes 7688 | tf_op jit(solution)/shard_map/ppermute | solution.py:34
  101.7 0.9 copy-start.30
  101.7 8.6 %copy-start.26 = (f32[16,40]{1,0:T(8,128)S(1)}, f32[16,40]{1,0:T(8,128)}, u32[]{:S(2)}) copy-start(f32[16,40]{1,0:T(8,128)} %and_convert_fusion) | copy-start | bytes 7684
  102.6 8.9 %collective-permute-start.11 = (f32[16,40]{1,0:T(8,128)S(1)}, f32[16,40]{1,0:T(8,128)}, u32[]{:S(2)}, u32[]{:S(2)}) collective-permute-start(f32[16,40]{1,0:T(8,128)S(1)} %slice_bitcast_fusion.7), channel_id=1, source_target_pairs={{0,256},{1,257},{2,258},{3,259},{4,260},{5,261},{6,262},{7,263},{8... | collective-permute-start | bytes 7688 | tf_op jit(solution)/shard_map/ppermute | solution.py:34
  111.5 1.8 %copy-start.4 = (f32[16,40,144]{1,0,2:T(8,128)}, f32[16,40,144]{1,0,2:T(8,128)S(1)}, u32[]{:S(2)}) copy-start(f32[16,40,144]{1,0,2:T(8,128)S(1)} %get-tuple-element.123) | copy-start | bytes 1105924 | tf_op jit(solution)/shard_map/cond
  120.8 8.4 %collective-permute-start.12 = (f32[4,8,32]{2,1,0:T(8,128)S(1)}, f32[4,8,32]{2,1,0:T(8,128)S(1)}, u32[]{:S(2)}, u32[]{:S(2)}) collective-permute-start(f32[4,8,32]{2,1,0:T(8,128)S(1)} %pad_maximum_fusion.9), channel_id=1, source_target_pairs={{256,0},{257,1},{258,2},{259,3},{260,4},{261,5},{262,6},{263,7},{2... | collective-permute-start | bytes 12296 | tf_op jit(solution)/shard_map/ppermute | solution.py:34
where the time goes:
time: 132 us; the launch traced here: 131 us
  starting transfers between devices  63.1 us (48%)
  local copies, waits for them, and re-layouts  36.8 us (28%)
  other arithmetic  23.4 us (18%)
  waiting for transfers between devices  6.17 us (5%)
    ppermute x5, starting transfers between devices, shifted(): return lax.ppermute(shard, axis, pairs)  30.6 us
    ppermute x4, starting transfers between devices, with_halo(): lax.ppermute(head, axis, [((i + 1) % count, i) for i in range(ends)])  20.9 us
    another operation x8, local copies, waits for them, and re-layouts  19.4 us
    add x4, other arithmetic, water_update(): 2.0 * field_now - field_old + TIME_STEP * TIME_STEP * moduli * laplace  13.3 us
    ppermute x4, starting transfers between devices, with_halo(): lax.ppermute(tail, axis, [(i, (i + 1) % count) for i in range(ends)])  11.6 us
    slice x4, local copies, waits for them, and re-layouts, from_above(): field[:, :, :-1]  6.57 us
    ppermute x5, waiting for transfers between devices, shifted(): return lax.ppermute(shard, axis, pairs)  5.52 us
    pad x4, local copies, waits for them, and re-layouts, advance(): padded = jnp.pad(field_now, ((1, 1), (1, 1), (0, 0)))  3.71 us
  transfers between devices with their start and end apart: 13, of which 4 were waited for; matrix products, arithmetic and copies ran while one was open for 8% of the time, Pallas kernels for 0%

commit v1 on v0

v1 whole, which is shorter than its diff:
```python
import functools

import jax
import jax.numpy as jnp
from jax import lax
from jax.experimental import pallas as pl
from jax.experimental.pallas import tpu as pltpu
from jax.sharding import PartitionSpec as P

STEPS = 4
PLANES = 144
THICK = PLANES // 3
TIME_STEP = 0.22
RELAXATION = 0.5
H2 = TIME_STEP * TIME_STEP

LANES = 128
ROWS = 16
PAD = 8
PERIOD = 9
MESH = pl.DeviceIdType.MESH
DIRS = tuple((dx, dy) for dx in (-1, 0, 1) for dy in (-1, 0, 1) if (dx, dy) != (0, 0))


def lanes_of(tile, count=1):
    start = (tile + PAD) * LANES
    if not isinstance(start, int):
        start = pl.multiple_of(start, LANES)
    return pl.ds(start, count * LANES)


def rows_sent(dx):
    return {0: pl.ds(0, 8), 1: pl.ds(4, 4), -1: pl.ds(0, 4)}[dx]


def rows_landed(dx):
    return {0: pl.ds(0, 8), 1: pl.ds(12, 4), -1: pl.ds(8, 4)}[dx]


def shift_x(value, by):
    return pltpu.roll(value, (-by) % ROWS, 0)


def turn(value, by):
    return pltpu.roll(value, (-by) % LANES, 1)


class Tiles:
    def __init__(self):
        self.known = {}

    def get(self, name, tile, make):
        key = (name, tile)
        if key not in self.known:
            self.known[key] = make()
        return self.known[key]


def flat_shift(memo, name, of, lane, tile, by):
    whole, part = divmod(by, LANES)
    first = memo.get(("turn", name, part), tile + whole, lambda: turn(of(tile + whole), part))
    if part == 0:
        return first
    second = memo.get(("turn", name, part), tile + whole + 1, lambda: turn(of(tile + whole + 1), part))
    return jnp.where(lane < LANES - part, first, second)


def seabed_block(src, old, dst, ca, cb, mod, kinds, zlow, zhigh, load, dst_pad, base, tiles, last):
    memo = Tiles()
    lane = lax.broadcasted_iota(jnp.int32, (ROWS, LANES), 1)
    rows = 8 if last else ROWS
    lane_out = lane[:rows]

    def at(ref, j):
        return ref[:, lanes_of(base + j)]

    def pattern(ref, j):
        return memo.get(id(ref), j % PERIOD, lambda: ref[:, pl.ds((j % PERIOD) * LANES, LANES)])

    def u(j):
        return memo.get("u", j, lambda: at(src, j))

    def zp(j):
        return memo.get("zp", j, lambda: flat_shift(memo, "u", u, lane, j, 1) * pattern(zhigh, j))

    def zm(j):
        return memo.get("zm", j, lambda: flat_shift(memo, "u", u, lane, j, -1) * pattern(zlow, j))

    def yp(j):
        return memo.get("yp", j, lambda: flat_shift(memo, "u", u, lane, j, PLANES))

    def ym(j):
        return memo.get("ym", j, lambda: flat_shift(memo, "u", u, lane, j, -PLANES))

    def slope_z(j):
        return memo.get("sz", j, lambda: zp(j) - zm(j))

    def slope_y(j):
        return memo.get("sy", j, lambda: yp(j) - ym(j))

    def cross_x(value):
        return (shift_x(value, 1) - shift_x(value, -1))[:rows]

    def cross_xy(j):
        return memo.get("xy", j, lambda: cross_x(slope_y(j)))

    def cross_xz(j):
        return memo.get("xz", j, lambda: cross_x(slope_z(j)))

    def slope_z_out(j):
        return memo.get("szo", j, lambda: slope_z(j)[:rows])

    def cross_yz(j):
        return memo.get(
            "yz", j,
            lambda: flat_shift(memo, "szo", slope_z_out, lane_out, j, PLANES)
            - flat_shift(memo, "szo", slope_z_out, lane_out, j, -PLANES),
        )

    def kind(j):
        return pattern(kinds, j)[:rows]

    def toward_low(j):
        return memo.get("w1", j, lambda: jnp.where(kind(j) == 1, cross_xy(j), cross_yz(j)))

    def toward_high(j):
        return memo.get("w2", j, lambda: jnp.where(kind(j) == 0, cross_xy(j), cross_yz(j)))

    out = {}
    for j in tiles:
        first, third = kind(j) == 0, kind(j) == 2
        from_high = flat_shift(memo, "w1", toward_low, lane_out, j, THICK)
        from_low = flat_shift(memo, "w2", toward_high, lane_out, j, -THICK)
        far_high = flat_shift(memo, "xz", cross_xz, lane_out, j, 2 * THICK)
        far_low = flat_shift(memo, "xz", cross_xz, lane_out, j, -2 * THICK)
        mixed = jnp.where(third, far_low, from_high) + jnp.where(first, far_high, from_low)
        lap_x = (shift_x(u(j), 1) + shift_x(u(j), -1))[:rows]
        lap_y = (yp(j) + ym(j))[:rows]
        lap_z = (zp(j) + zm(j))[:rows]
        centre = u(j)[:rows]
        twice = centre + centre
        own = jnp.where(first, lap_x, jnp.where(third, lap_z, lap_y)) - twice
        lap = lap_x + lap_y + lap_z - 6.0 * centre
        acc = at(ca, j)[:rows] * (own + 0.25 * mixed) + at(cb, j)[:rows] * lap
        pushed = load(j)
        if pushed is not None:
            acc = acc + (H2 * at(mod, j)[:rows]) * pushed[:rows]
        new = twice - at(old, j)[:rows] + acc
        if last:
            dst[:, pl.ds(dst_pad + j * LANES, LANES)] = new
        else:
            dst[:, lanes_of(base + j)] = new
        out[j] = acc
    return out


def water_block(src, old, dst, mod, ghost, dst_pad, base, tiles, last):
    memo = Tiles()
    lane = lax.broadcasted_iota(jnp.int32, (ROWS, LANES), 1)
    rows = 8 if last else ROWS

    def at(ref, j):
        return ref[:, lanes_of(base + j)]

    def u(j):
        return memo.get("u", j, lambda: at(src, j))

    for j in tiles:
        below = flat_shift(memo, "u", u, lane, j, 1)
        above = flat_shift(memo, "u", u, lane, j, -1)
        offset = (j * LANES) % PLANES
        top = (-offset) % PLANES
        floor = PLANES - 1 - offset
        if top < LANES:
            above = jnp.where(lane == top, 0.0, above)
        if 0 <= floor < LANES:
            below = jnp.where(lane == floor, u(j) - ghost(j), below)
        total = (shift_x(u(j), 1) + shift_x(u(j), -1)) + (below + above)
        total = total + (flat_shift(memo, "u", u, lane, j, PLANES) + flat_shift(memo, "u", u, lane, j, -PLANES))
        total = (total - 6.0 * u(j))[:rows]
        centre = u(j)[:rows]
        new = (centre + centre) - at(old, j)[:rows] + (H2 * at(mod, j)[:rows]) * total
        if last:
            dst[:, pl.ds(dst_pad + j * LANES, LANES)] = new
        else:
            dst[:, lanes_of(base + j)] = new


def floor_lane(tile):
    if tile % PERIOD == 0:
        return None
    return (tile - 1) // PERIOD, 16 * ((tile - 1) % PERIOD) + 15


def top_lane(tile):
    place = {0: 0, 1: 1, 3: 2, 4: 3, 5: 4, 6: 5, 7: 6, 8: 7}.get(tile % PERIOD)
    if place is None:
        return None
    return tile // PERIOD, (16 * place + 2 * THICK) % LANES


def exact_dot(a, b):
    return jnp.dot(a, b, precision=lax.Precision.HIGHEST, preferred_element_type=jnp.float32)


def kernel(
    sizes, own_tiles, cur_hbm, prev_hbm, mat_hbm, prior_hbm, fields_ref, floor_ref,
    cur, prev, mat, p1, p2, p3, ca, cb, kinds, zlow, zhigh, prior, rims, packed, arrived, spread, columns, moved, returned,
    load_sem, send_sem, recv_sem, prior_send, prior_recv, trace_send, trace_recv, move_send, move_recv,
):
    half, gx, gy = lax.axis_index("half"), lax.axis_index("gx"), lax.axis_index("gy")
    n_x, n_y = sizes
    wet = half == 0
    groups = own_tiles // PERIOD

    def exists(dx, dy):
        x, y = gx + dx, gy + dy
        return (x >= 0) & (x < n_x) & (y >= 0) & (y < n_y)

    loads = [
        pltpu.make_async_copy(src.at[0], dst.at[0:8, lanes_of(0, own_tiles)], load_sem.at[n])
        for n, (src, dst) in enumerate(((cur_hbm, cur), (prev_hbm, prev), (mat_hbm, mat)))
    ]
    loads.append(pltpu.make_async_copy(prior_hbm, prior, load_sem.at[3]))
    for copy in loads:
        copy.start()

    barrier = pltpu.get_barrier_semaphore()
    count = jnp.int32(1)
    for dx, dy in DIRS:
        here = exists(dx, dy)
        count = count + here.astype(jnp.int32)

        @pl.when(here)
        def _(dx=dx, dy=dy):
            pl.semaphore_signal(barrier, inc=1, device_id={"gx": gx + dx, "gy": gy + dy}, device_id_type=MESH)

    pl.semaphore_signal(barrier, inc=1, device_id={"half": 1 - half}, device_id_type=MESH)

    flat = lax.broadcasted_iota(jnp.int32, (ROWS, PERIOD * LANES), 1)
    plane = flat % PLANES
    part = plane // THICK
    level = plane - part * THICK
    kinds[...] = part
    zlow[...] = (level != 0).astype(jnp.float32)
    zhigh[...] = (level != THICK - 1).astype(jnp.float32)

    def halo_copies(dx, dy):
        out = []
        for n, (ref, width) in enumerate(((cur, 5), (prev, 4), (mat, 4))):
            if dy == 0:
                src_lanes = dst_lanes = lanes_of(0, own_tiles)
            elif dy == 1:
                src_lanes, dst_lanes = lanes_of(own_tiles - width, width), lanes_of(-width, width)
            else:
                src_lanes, dst_lanes = lanes_of(0, width), lanes_of(own_tiles, width)
            slot = DIRS.index((dx, dy)) * 3 + n
            out.append(
                pltpu.make_async_remote_copy(
                    src_ref=ref.at[rows_sent(dx), src_lanes],
                    dst_ref=ref.at[rows_landed(dx), dst_lanes],
                    send_sem=send_sem.at[slot],
                    recv_sem=recv_sem.at[slot],
                    device_id={"gx": gx + dx, "gy": gy + dy},
                    device_id_type=MESH,
                )
            )
        return out

    def prior_copy(dx, dy):
        slot = DIRS.index((dx, dy))
        return pltpu.make_async_remote_copy(
            src_ref=prior.at[pl.ds(0, STEPS - 1)],
            dst_ref=rims.at[slot],
            send_sem=prior_send.at[slot],
            recv_sem=prior_recv.at[slot],
            device_id={"gx": gx + dx, "gy": gy + dy},
            device_id_type=MESH,
        )

    blank = jnp.zeros((ROWS, LANES), jnp.float32)
    for ref, reach in ((mat, 5), (p1, 5), (p2, 4), (p3, 3)):
        ref[:, lanes_of(-reach)] = blank
        ref[:, lanes_of(own_tiles + reach - 1)] = blank

    for dx, dy in DIRS:
        @pl.when(jnp.logical_not(exists(-dx, -dy)))
        def _(dx=dx, dy=dy):
            lanes = {0: lanes_of(0, own_tiles), 1: lanes_of(-5, 5), -1: lanes_of(own_tiles, 5)}[dy]
            for ref in (cur, prev, mat):
                ref[rows_landed(dx), lanes] = jnp.zeros((8 if dx == 0 else 4, lanes.size), jnp.float32)
            rims[DIRS.index((dx, dy))] = jnp.zeros(rims.shape[1:], jnp.float32)

    for copy in loads:
        copy.wait()
    pl.semaphore_wait(barrier, count)

    order = sorted(DIRS, key=lambda d: (d[1] == 0, d[0] != 0))
    for dx, dy in order:
        @pl.when(exists(dx, dy))
        def _(dx=dx, dy=dy):
            for copy in halo_copies(dx, dy):
                copy.start()

            @pl.when(wet)
            def _():
                prior_copy(dx, dy).start()

    for dx, dy in DIRS:
        @pl.when(exists(-dx, -dy))
        def _(dx=dx, dy=dy):
            for copy in halo_copies(dx, dy):
                copy.wait_recv()

            @pl.when(wet)
            def _():
                prior_copy(dx, dy).wait_recv()

    lane = lax.broadcasted_iota(jnp.int32, (ROWS, LANES), 1)
    levels = (cur, p1, p2, p3)
    olds = (prev, cur, p1, p2)
    width = own_tiles * LANES

    def over_tiles(block, t):
        margin = STEPS - 1 - t
        edge = -(-margin * PLANES // LANES)
        if edge:
            block(0, range(-edge, 0), 0)
        @pl.loop(0, groups)
        def _(g):
            block(g * PERIOD, range(PERIOD), g + 1)

        if edge:
            block(own_tiles, range(edge), groups + 1)

    def trace_copy(t):
        return pltpu.make_async_remote_copy(
            src_ref=packed.at[t], dst_ref=arrived.at[t], send_sem=trace_send.at[t], recv_sem=trace_recv.at[t],
            device_id={"half": 1 - half}, device_id_type=MESH,
        )

    def move_copy(t):
        return pltpu.make_async_remote_copy(
            src_ref=moved.at[t], dst_ref=returned.at[t], send_sem=move_send.at[t], recv_sem=move_recv.at[t],
            device_id={"half": 1 - half}, device_id_type=MESH,
        )

    def dense(value, first):
        cells = 8 * groups
        row = lax.broadcasted_iota(jnp.int32, (LANES, cells), 0)
        col = lax.broadcasted_iota(jnp.int32, (LANES, cells), 1)
        pick = (row == 16 * (col % 8) + first + col // 8).astype(jnp.float32)
        return exact_dot(value, pick)

    @pl.when(wet)
    def _():
        cells = 8 * groups
        row = lax.broadcasted_iota(jnp.int32, (cells, groups * LANES), 0)
        col = lax.broadcasted_iota(jnp.int32, (cells, groups * LANES), 1)
        place = (col == LANES * (row // 8) + 16 * (row % 8) + 15).astype(jnp.float32)
        upper = lax.broadcasted_iota(jnp.int32, (8, cells), 0) < 4

        def rim(dx, dy, t):
            return rims[DIRS.index((dx, dy)), t]

        for t in range(STEPS):
            centre = prior[t]
            if t == STEPS - 1:
                spread[t, 0:8, pl.ds(LANES, groups * LANES)] = exact_dot(centre, place)
                continue
            for dy, value in (
                (0, jnp.concatenate([centre, jnp.where(upper, rim(-1, 0, t), rim(1, 0, t))], 0)),
                (1, jnp.concatenate([rim(0, 1, t), jnp.where(upper, rim(-1, 1, t), rim(1, 1, t))], 0)),
                (-1, jnp.concatenate([rim(0, -1, t), jnp.where(upper, rim(-1, -1, t), rim(1, -1, t))], 0)),
            ):
                if dy == 0:
                    spread[t, :, pl.ds(LANES, groups * LANES)] = exact_dot(value, place)
                elif dy == 1:
                    spread[t, :, pl.ds(0, LANES)] = exact_dot(value, place[:, (groups - 1) * LANES:])
                else:
                    spread[t, :, pl.ds((groups + 1) * LANES, LANES)] = exact_dot(value, place[:, :LANES])

        for t in range(STEPS):
            src, old = levels[t], olds[t]
            margin = STEPS - 1 - t
            total = None
            for g in range(-1, groups + 1):
                tile = None
                for j in range(8):
                    q = g * PERIOD + j + 1
                    edge = -(-margin * PLANES // LANES)
                    if q < -edge or q >= own_tiles + edge:
                        continue
                    value = src[:, lanes_of(q)]
                    tile = value if tile is None else jnp.where(lane == 16 * j + 15, value, tile)
                if tile is None:
                    continue
                tile = jnp.where(lane % 16 == 15, tile, 0.0)
                tile = turn(tile, 15 - (g + 1))
                total = tile if total is None else total + tile
            packed[t] = total
            trace_copy(t).start()

            def block(base, tiles, slot, t=t, src=src, old=old):
                last = t == STEPS - 1
                start = 0
                if last:
                    start = pl.multiple_of(base * LANES, LANES)

                def ghost(j):
                    at = slot * LANES
                    if not isinstance(at, int):
                        at = pl.multiple_of(at, LANES)
                    return spread[t, :, pl.ds(at, LANES)]

                dst = fields_ref.at[0] if last else levels[t + 1]
                water_block(src, old, dst, mat, ghost, start, base, tiles, last)

            over_tiles(block, t)

        for t in range(STEPS):
            move_copy(t).wait_recv()
            floor_ref[0, t] = RELAXATION * dense(returned[t], 0) + (1.0 - RELAXATION) * prior[t]
            trace_copy(t).wait_send()

    @pl.when(jnp.logical_not(wet))
    def _():
        def moduli(base, tiles, slot):
            memo = Tiles()

            def m(j):
                return memo.get("m", j, lambda: mat[:, lanes_of(base + j)])

            for j in tiles:
                which = kinds[:, pl.ds((j % PERIOD) * LANES, LANES)]
                first, third = which == 0, which == 2
                up1 = flat_shift(memo, "m", m, lane, j, THICK)
                up2 = flat_shift(memo, "m", m, lane, j, 2 * THICK)
                down1 = flat_shift(memo, "m", m, lane, j, -THICK)
                down2 = flat_shift(memo, "m", m, lane, j, -2 * THICK)
                bulk = jnp.where(first, m(j), jnp.where(third, down2, down1))
                shear = jnp.where(first, up1, jnp.where(third, down1, m(j)))
                light = H2 * jnp.where(first, up2, jnp.where(third, m(j), up1))
                ca[:, lanes_of(base + j)] = light * bulk
                cb[:, lanes_of(base + j)] = light * shear

        over_tiles(moduli, 0)

        for t in range(STEPS):
            src, old = levels[t], olds[t]
            last = t == STEPS - 1
            trace_copy(t).wait_recv()
            for g in range(-1, groups + 1):
                spread[t, :, pl.ds((g + 1) * LANES, LANES)] = turn(arrived[t], (g + 1) - 2 * THICK)

            def block(base, tiles, slot, t=t, src=src, old=old, last=last):
                start = pl.multiple_of(base * LANES, LANES) if last else 0

                def load(j):
                    spot = top_lane(j)
                    if spot is None:
                        return None
                    at = slot * LANES
                    if not isinstance(at, int):
                        at = pl.multiple_of(at, LANES)
                    value = spread[t, :, pl.ds(at, LANES)]
                    return jnp.where(lane == spot[1], value, 0.0)

                dst = fields_ref.at[0] if last else levels[t + 1]
                acc = seabed_block(
                    src, old, dst, ca, cb, mat, kinds, zlow, zhigh, load, start, base, tiles, last
                )
                if len(tiles) == PERIOD:
                    tile = None
                    for j in tiles:
                        spot = top_lane(j)
                        if spot is not None:
                            value = acc[j][:8]
                            tile = value if tile is None else jnp.where(lane[:8] == spot[1], value, tile)
                    at = pl.multiple_of((slot - 1) * LANES, LANES)
                    columns[:, pl.ds(at, LANES)] = tile

            over_tiles(block, t)
            total = None
            for g in range(groups):
                tile = columns[:, pl.ds(g * LANES, LANES)] * (1.0 / H2)
                tile = turn(jnp.where(lane[:8] % 16 == 0, tile, 0.0), 2 * THICK - g)
                total = tile if total is None else total + tile
            moved[t] = total
            move_copy(t).start()

        for t in range(STEPS):
            floor_ref[0, t] = dense(arrived[t, 0:8], 1)
            move_copy(t).wait_send()

    for dx, dy in DIRS:
        @pl.when(exists(dx, dy))
        def _(dx=dx, dy=dy):
            for copy in halo_copies(dx, dy):
                copy.wait_send()

            @pl.when(wet)
            def _():
                prior_copy(dx, dy).wait_send()


def on_device(sizes, current, previous, material, prior):
    own = current.shape[2]
    own_tiles = own // LANES
    groups = own_tiles // PERIOD
    cells = own // PLANES
    field = pltpu.VMEM((ROWS, (own_tiles + 2 * PAD) * LANES), jnp.float32)
    pattern = pltpu.VMEM((ROWS, PERIOD * LANES), jnp.float32)
    anywhere = pl.BlockSpec(memory_space=pl.ANY)
    near = pl.BlockSpec(memory_space=pltpu.VMEM)
    dma = pltpu.SemaphoreType.DMA
    return pl.pallas_call(
        functools.partial(kernel, sizes, own_tiles),
        out_shape=(
            jax.ShapeDtypeStruct(current.shape, jnp.float32),
            jax.ShapeDtypeStruct((1,) + prior.shape, jnp.float32),
        ),
        in_specs=[anywhere] * 4,
        out_specs=(near, near),
        scratch_shapes=[field] * 8
        + [
            pltpu.VMEM((ROWS, PERIOD * LANES), jnp.int32),
            pattern,
            pattern,
            pltpu.VMEM(prior.shape, jnp.float32),
            pltpu.VMEM((len(DIRS), STEPS - 1) + prior.shape[1:], jnp.float32),
            pltpu.VMEM((STEPS, ROWS, LANES), jnp.float32),
            pltpu.VMEM((STEPS, ROWS, LANES), jnp.float32),
            pltpu.VMEM((STEPS, ROWS, (groups + 2) * LANES), jnp.float32),
            pltpu.VMEM((8, groups * LANES), jnp.float32),
            pltpu.VMEM((STEPS, 8, LANES), jnp.float32),
            pltpu.VMEM((STEPS, 8, LANES), jnp.float32),
            dma((4,)),
            dma((3 * len(DIRS),)),
            dma((3 * len(DIRS),)),
            dma((len(DIRS),)),
            dma((len(DIRS),)),
            dma((STEPS,)),
            dma((STEPS,)),
            dma((STEPS,)),
            dma((STEPS,)),
        ],
        compiler_params=pltpu.CompilerParams(collective_id=0, has_side_effects=True),
    )(current, previous, material, prior)


def solution(mesh):
    placed = (
        P("half", "gx", "gy"),
        P("half", "gx", "gy"),
        P("half", "gx", "gy"),
        P(None, "gx", "gy"),
    )
    return jax.shard_map(
        functools.partial(on_device, (mesh.shape["gx"], mesh.shape["gy"])),
        mesh=mesh,
        in_specs=placed,
        out_specs=(P("half", "gx", "gy"), P("half", None, "gx", "gy")),
        check_vma=False,
    )
```

time: 132 us -> 34.5 us (0.26)
  the two profiles are of different devices: /device:TPU:288 before, /device:TPU:216 now
where the time goes in v1:
time: 34.5 us; the launch traced here: 34.4 us
  Pallas kernels  31.5 us (91%)
  local copies, waits for them, and re-layouts  2.2 us (6%)
  between operations  0.65 us (2%)
    pallas_call x1, Pallas kernels, on_device(): pl.pallas_call(functools.partial(kernel, sizes, own_tiles), out_shape=(ja...  31.5 us
    unnamed x4, local copies, waits for them, and re-layouts  2.2 us

profile of v1, /device:TPU:216, one launch (start us, length us, event | category | flops | bytes accessed | tf_op | source)
XLA Modules:
  0.0 34.4 jit_solution(15408098136768280778)
XLA Ops:
  0.6 31.5 %shard_map.59 = (f32[1,8,4608]{2,1,0:T(8,128)}, f32[1,4,8,32]{3,2,1,0:T(8,128)}) custom-call(f32[1,8,4608]{2,1,0:T(8,128)} %cur_hbm.1, f32[1,8,4608]{2,1,0:T(8,128)} %prev_hbm.1, f32[1,8,4608]{2,1,0:T(8,128)} %mat_hbm.1, f32[4,8,32]{2,1,0:T(8,128)} %prior_hbm.1), custom_call_target="tpu_custom_call" | custom-call | tf_op jit(solution)/shard_map/pallas_call | solution.py:517
  32.2 0.0 copy-start
  32.2 1.6 %copy.8 = f32[1,8,4608]{2,1,0:T(8,128)} copy(f32[1,8,4608]{2,1,0:T(8,128)} %get-tuple-element.4) | data formatting | bytes 294912
  33.8 0.0 copy-done
  33.8 0.6 %copy.9 = f32[1,4,8,32]{3,2,1,0:T(8,128)} copy(f32[1,4,8,32]{3,2,1,0:T(8,128)S(1)} %copy-done) | data formatting | bytes 8192
Async XLA Ops:
  32.2 1.6 %copy-start = (f32[1,4,8,32]{3,2,1,0:T(8,128)S(1)}, f32[1,4,8,32]{3,2,1,0:T(8,128)}, u32[]{:S(2)}) copy-start(f32[1,4,8,32]{3,2,1,0:T(8,128)} %get-tuple-element.5) | copy-start | bytes 12292

commit v2 on v1

--- a/solution.py
+++ b/solution.py
@@ -17,6 +17,9 @@
 LANES = 128
 ROWS = 16
 PAD = 8
+SPAN = 2
+HALVES = 16
+SLOTS = HALVES + 2 * STEPS
 PERIOD = 9
 MESH = pl.DeviceIdType.MESH
 DIRS = tuple((dx, dy) for dx in (-1, 0, 1) for dy in (-1, 0, 1) if (dx, dy) != (0, 0))
@@ -65,93 +68,96 @@
     return jnp.where(lane < LANES - part, first, second)
 
 
-def seabed_block(src, old, dst, ca, cb, mod, kinds, zlow, zhigh, load, dst_pad, base, tiles, last):
+def unit_window(memo, of, lane, start, low, high):
+    tile, part = divmod(start, LANES)
+    if part + low >= LANES:
+        tile, part, low, high = tile + 1, part - LANES, low, high
+    first = memo.get("turn", (tile, part % LANES), lambda: turn(of(tile), part % LANES))
+    if part + high <= LANES:
+        return first
+    second = memo.get("turn", (tile + 1, part % LANES), lambda: turn(of(tile + 1), part % LANES))
+    return jnp.where(lane < LANES - part, first, second)
+
+
+def to_planes(ref, rows, slots, base, store):
     memo = Tiles()
+    lane = lax.broadcasted_iota(jnp.int32, (8, LANES), 1)
+
+    def of(tile):
+        return memo.get("load", tile, lambda: ref[rows, lanes_of(base + tile)])
+
+    for slot in slots:
+        parts = []
+        for c in range(3):
+            near = (slot - STEPS) * PLANES + c * THICK
+            far = near + HALVES * PLANES - THICK
+            parts.append(
+                jnp.where(
+                    lane < THICK,
+                    unit_window(memo, of, lane, near, 0, THICK),
+                    unit_window(memo, of, lane, far, THICK, 2 * THICK),
+                )
+            )
+        store(slot, parts)
+
+
+def from_planes(planes, dst, tiles):
+    lane = lax.broadcasted_iota(jnp.int32, (8, LANES), 1)
+    for q in tiles:
+        out = None
+        for n in range(q * LANES // THICK, (q * LANES + LANES - 1) // THICK + 1):
+            cell, c = divmod(n, 3)
+            far = cell >= HALVES
+            slot = cell + STEPS - (HALVES if far else 0)
+            value = turn(planes[slot, c, 0:8], q * LANES - n * THICK + (THICK if far else 0))
+            out = value if out is None else jnp.where(lane < n * THICK - q * LANES, out, value)
+        dst[:, pl.ds(q * LANES, LANES)] = out
+
+
+def slopes(src, level, slot, sz, sx, ex, ez, lap, rows):
     lane = lax.broadcasted_iota(jnp.int32, (ROWS, LANES), 1)
-    rows = 8 if last else ROWS
-    lane_out = lane[:rows]
-
-    def at(ref, j):
-        return ref[:, lanes_of(base + j)]
-
-    def pattern(ref, j):
-        return memo.get(id(ref), j % PERIOD, lambda: ref[:, pl.ds((j % PERIOD) * LANES, LANES)])
-
-    def u(j):
-        return memo.get("u", j, lambda: at(src, j))
-
-    def zp(j):
-        return memo.get("zp", j, lambda: flat_shift(memo, "u", u, lane, j, 1) * pattern(zhigh, j))
-
-    def zm(j):
-        return memo.get("zm", j, lambda: flat_shift(memo, "u", u, lane, j, -1) * pattern(zlow, j))
-
-    def yp(j):
-        return memo.get("yp", j, lambda: flat_shift(memo, "u", u, lane, j, PLANES))
-
-    def ym(j):
-        return memo.get("ym", j, lambda: flat_shift(memo, "u", u, lane, j, -PLANES))
-
-    def slope_z(j):
-        return memo.get("sz", j, lambda: zp(j) - zm(j))
-
-    def slope_y(j):
-        return memo.get("sy", j, lambda: yp(j) - ym(j))
-
-    def cross_x(value):
-        return (shift_x(value, 1) - shift_x(value, -1))[:rows]
-
-    def cross_xy(j):
-        return memo.get("xy", j, lambda: cross_x(slope_y(j)))
-
-    def cross_xz(j):
-        return memo.get("xz", j, lambda: cross_x(slope_z(j)))
-
-    def slope_z_out(j):
-        return memo.get("szo", j, lambda: slope_z(j)[:rows])
-
-    def cross_yz(j):
-        return memo.get(
-            "yz", j,
-            lambda: flat_shift(memo, "szo", slope_z_out, lane_out, j, PLANES)
-            - flat_shift(memo, "szo", slope_z_out, lane_out, j, -PLANES),
-        )
-
-    def kind(j):
-        return pattern(kinds, j)[:rows]
-
-    def toward_low(j):
-        return memo.get("w1", j, lambda: jnp.where(kind(j) == 1, cross_xy(j), cross_yz(j)))
-
-    def toward_high(j):
-        return memo.get("w2", j, lambda: jnp.where(kind(j) == 0, cross_xy(j), cross_yz(j)))
-
-    out = {}
-    for j in tiles:
-        first, third = kind(j) == 0, kind(j) == 2
-        from_high = flat_shift(memo, "w1", toward_low, lane_out, j, THICK)
-        from_low = flat_shift(memo, "w2", toward_high, lane_out, j, -THICK)
-        far_high = flat_shift(memo, "xz", cross_xz, lane_out, j, 2 * THICK)
-        far_low = flat_shift(memo, "xz", cross_xz, lane_out, j, -2 * THICK)
-        mixed = jnp.where(third, far_low, from_high) + jnp.where(first, far_high, from_low)
-        lap_x = (shift_x(u(j), 1) + shift_x(u(j), -1))[:rows]
-        lap_y = (yp(j) + ym(j))[:rows]
-        lap_z = (zp(j) + zm(j))[:rows]
-        centre = u(j)[:rows]
-        twice = centre + centre
-        own = jnp.where(first, lap_x, jnp.where(third, lap_z, lap_y)) - twice
-        lap = lap_x + lap_y + lap_z - 6.0 * centre
-        acc = at(ca, j)[:rows] * (own + 0.25 * mixed) + at(cb, j)[:rows] * lap
-        pushed = load(j)
-        if pushed is not None:
-            acc = acc + (H2 * at(mod, j)[:rows]) * pushed[:rows]
-        new = twice - at(old, j)[:rows] + acc
-        if last:
-            dst[:, pl.ds(dst_pad + j * LANES, LANES)] = new
-        else:
-            dst[:, lanes_of(base + j)] = new
-        out[j] = acc
-    return out
+    keep_up = jnp.where((lane == THICK - 1) | (lane >= 2 * THICK - 1), 0.0, 1.0)
+    keep_down = jnp.where((lane == 0) | (lane == THICK), 0.0, 1.0)
+    lap_x, lap_z, mixed = [], [], []
+    for c in range(3):
+        u = src[slot, c]
+        up, down = turn(u, 1) * keep_up, turn(u, -1) * keep_down
+        right, left = shift_x(u, 1)[:rows], shift_x(u, -1)[:rows]
+        slope_z = (up - down) * 0.25
+        lap_z.append((up + down)[:rows])
+        lap_x.append(right + left)
+        if c < 2:
+            sx[level, slot, c, 0:rows] = (right - left) * 0.25
+        if c > 0:
+            sz[level, slot, c - 1, 0:rows] = slope_z[:rows]
+        if c != 1:
+            mixed.append((shift_x(slope_z, 1) - shift_x(slope_z, -1))[:rows])
+        lap[level, slot, c, 0:rows] = lap_x[c] + lap_z[c]
+    ex[level, slot, 0:rows] = lap_x[0] + mixed[1]
+    ez[level, slot, 0:rows] = lap_z[2] + mixed[0]
+
+
+def advance_slot(src, old, dst, level, slot, sz, sx, ex, ez, lap, stiff, pushed, rows):
+    bulk, shear, light = (stiff[slot, n, 0:rows] for n in range(3))
+    centre = [src[slot, c, 0:rows] for c in range(3)]
+    lap_y = [src[slot + 1, c, 0:rows] + src[slot - 1, c, 0:rows] for c in range(3)]
+
+    def along(ref, c):
+        return ref[level, slot + 1, c, 0:rows] - ref[level, slot - 1, c, 0:rows]
+
+    grad = (
+        ex[level, slot, 0:rows] + along(sx, 1),
+        lap_y[1] + (along(sx, 0) + along(sz, 1)),
+        ez[level, slot, 0:rows] + along(sz, 0),
+    )
+    for c in range(3):
+        twice = centre[c] + centre[c]
+        total = lap[level, slot, c, 0:rows] + lap_y[c] - 6.0 * centre[c]
+        acc = bulk * (grad[c] - twice) + shear * total
+        if c == 2:
+            acc = acc + light * pushed
+        dst[slot, c, 0:rows] = twice - old[slot, c, 0:rows] + acc
+    return acc
 
 
 def water_block(src, old, dst, mod, ghost, dst_pad, base, tiles, last):
@@ -192,20 +198,14 @@
     return (tile - 1) // PERIOD, 16 * ((tile - 1) % PERIOD) + 15
 
 
-def top_lane(tile):
-    place = {0: 0, 1: 1, 3: 2, 4: 3, 5: 4, 6: 5, 7: 6, 8: 7}.get(tile % PERIOD)
-    if place is None:
-        return None
-    return tile // PERIOD, (16 * place + 2 * THICK) % LANES
-
-
 def exact_dot(a, b):
     return jnp.dot(a, b, precision=lax.Precision.HIGHEST, preferred_element_type=jnp.float32)
 
 
 def kernel(
     sizes, own_tiles, cur_hbm, prev_hbm, mat_hbm, prior_hbm, fields_ref, floor_ref,
-    cur, prev, mat, p1, p2, p3, ca, cb, kinds, zlow, zhigh, prior, rims, packed, arrived, spread, columns, moved, returned,
+    cur, prev, mat, p1, p2, p3, d0, d1, d2, d3, d4, before, stiff, sz, sx, ex, ez, lap,
+    prior, rims, packed, arrived, spread, moved, returned,
     load_sem, send_sem, recv_sem, prior_send, prior_recv, trace_send, trace_recv, move_send, move_recv,
 ):
     half, gx, gy = lax.axis_index("half"), lax.axis_index("gx"), lax.axis_index("gy")
@@ -236,14 +236,6 @@
             pl.semaphore_signal(barrier, inc=1, device_id={"gx": gx + dx, "gy": gy + dy}, device_id_type=MESH)
 
     pl.semaphore_signal(barrier, inc=1, device_id={"half": 1 - half}, device_id_type=MESH)
-
-    flat = lax.broadcasted_iota(jnp.int32, (ROWS, PERIOD * LANES), 1)
-    plane = flat % PLANES
-    part = plane // THICK
-    level = plane - part * THICK
-    kinds[...] = part
-    zlow[...] = (level != 0).astype(jnp.float32)
-    zhigh[...] = (level != THICK - 1).astype(jnp.float32)
 
     def halo_copies(dx, dy):
         out = []
@@ -278,11 +270,6 @@
             device_id_type=MESH,
         )
 
-    blank = jnp.zeros((ROWS, LANES), jnp.float32)
-    for ref, reach in ((mat, 5), (p1, 5), (p2, 4), (p3, 3)):
-        ref[:, lanes_of(-reach)] = blank
-        ref[:, lanes_of(own_tiles + reach - 1)] = blank
-
     for dx, dy in DIRS:
         @pl.when(jnp.logical_not(exists(-dx, -dy)))
         def _(dx=dx, dy=dy):
@@ -420,75 +407,74 @@
 
         for t in range(STEPS):
             move_copy(t).wait_recv()
-            floor_ref[0, t] = RELAXATION * dense(returned[t], 0) + (1.0 - RELAXATION) * prior[t]
+            motion = jnp.where(lane[:8] < HALVES, returned[t], turn(returned[t], THICK - HALVES))
+            floor_ref[0, t] = RELAXATION * motion[:, : 8 * groups] + (1.0 - RELAXATION) * prior[t]
             trace_copy(t).wait_send()
 
     @pl.when(jnp.logical_not(wet))
     def _():
-        def moduli(base, tiles, slot):
-            memo = Tiles()
-
-            def m(j):
-                return memo.get("m", j, lambda: mat[:, lanes_of(base + j)])
-
-            for j in tiles:
-                which = kinds[:, pl.ds((j % PERIOD) * LANES, LANES)]
-                first, third = which == 0, which == 2
-                up1 = flat_shift(memo, "m", m, lane, j, THICK)
-                up2 = flat_shift(memo, "m", m, lane, j, 2 * THICK)
-                down1 = flat_shift(memo, "m", m, lane, j, -THICK)
-                down2 = flat_shift(memo, "m", m, lane, j, -2 * THICK)
-                bulk = jnp.where(first, m(j), jnp.where(third, down2, down1))
-                shear = jnp.where(first, up1, jnp.where(third, down1, m(j)))
-                light = H2 * jnp.where(first, up2, jnp.where(third, m(j), up1))
-                ca[:, lanes_of(base + j)] = light * bulk
-                cb[:, lanes_of(base + j)] = light * shear
-
-        over_tiles(moduli, 0)
+        def convert(rows, slots, base=0, shift=0):
+            def put(ref):
+                def store(slot, parts):
+                    for c in range(3):
+                        ref[slot + shift, c, rows] = parts[c]
+                return store
+
+            def put_stiff(slot, parts):
+                light = H2 * parts[2]
+                stiff[slot + shift, 0, rows] = light * parts[0]
+                stiff[slot + shift, 1, rows] = light * parts[1]
+                stiff[slot + shift, 2, rows] = light
+
+            inner = [slot for slot in slots if 0 < slot < SLOTS - 1]
+            to_planes(cur, rows, slots, base, put(d0))
+            to_planes(prev, rows, inner, base, put(before))
+            to_planes(mat, rows, inner, base, put_stiff)
+
+        for rows in (pl.ds(0, 8), pl.ds(8, 8)):
+            @pl.loop(0, HALVES // 8)
+            def _(n, rows=rows):
+                convert(rows, range(STEPS, STEPS + 8), n * PERIOD, n * 8)
+
+            convert(rows, (*range(STEPS), *range(SLOTS - STEPS, SLOTS)))
+
+        displaced = (d0, d1, d2, d3, d4)
+        earlier = (before, d0, d1, d2)
+        scratch = (sz, sx, ex, ez, lap)
+        lane8 = lane[:8]
 
         for t in range(STEPS):
-            src, old = levels[t], olds[t]
             last = t == STEPS - 1
+            rows = 8 if last else ROWS
+            src, old, dst = displaced[t], earlier[t], displaced[t + 1]
+
+            @pl.loop(t, SLOTS - t, step=SPAN)
+            def _(first, t=t, src=src, rows=rows):
+                for k in range(SPAN):
+                    slopes(src, t, first + k, *scratch, rows)
+
             trace_copy(t).wait_recv()
-            for g in range(-1, groups + 1):
-                spread[t, :, pl.ds((g + 1) * LANES, LANES)] = turn(arrived[t], (g + 1) - 2 * THICK)
-
-            def block(base, tiles, slot, t=t, src=src, old=old, last=last):
-                start = pl.multiple_of(base * LANES, LANES) if last else 0
-
-                def load(j):
-                    spot = top_lane(j)
-                    if spot is None:
-                        return None
-                    at = slot * LANES
-                    if not isinstance(at, int):
-                        at = pl.multiple_of(at, LANES)
-                    value = spread[t, :, pl.ds(at, LANES)]
-                    return jnp.where(lane == spot[1], value, 0.0)
-
-                dst = fields_ref.at[0] if last else levels[t + 1]
-                acc = seabed_block(
-                    src, old, dst, ca, cb, mat, kinds, zlow, zhigh, load, start, base, tiles, last
+            load = arrived[t][:rows]
+            lane_out = lane[:rows]
+
+            def pushed(slot, load=load, lane_out=lane_out):
+                cell = slot - STEPS
+                near = cell % 8 * 16 + 1 + cell // 8
+                return jnp.where(
+                    lane_out == 0, turn(load, near),
+                    jnp.where(lane_out == THICK, turn(load, near + HALVES // 8 - THICK), 0.0),
                 )
-                if len(tiles) == PERIOD:
-                    tile = None
-                    for j in tiles:
-                        spot = top_lane(j)
-                        if spot is not None:
-                            value = acc[j][:8]
-                            tile = value if tile is None else jnp.where(lane[:8] == spot[1], value, tile)
-                    at = pl.multiple_of((slot - 1) * LANES, LANES)
-                    columns[:, pl.ds(at, LANES)] = tile
-
-            over_tiles(block, t)
-            total = None
-            for g in range(groups):
-                tile = columns[:, pl.ds(g * LANES, LANES)] * (1.0 / H2)
-                tile = turn(jnp.where(lane[:8] % 16 == 0, tile, 0.0), 2 * THICK - g)
-                total = tile if total is None else total + tile
-            moved[t] = total
+
+            total = jnp.zeros((8, LANES), jnp.float32)
+            for slot in range(t + 1, SLOTS - 1 - t):
+                acc = advance_slot(src, old, dst, t, slot, *scratch, stiff, pushed(slot), rows)
+                cell = slot - STEPS
+                if 0 <= cell < HALVES:
+                    total = jnp.where((lane8 == cell) | (lane8 == THICK + cell), turn(acc[:8], -cell), total)
+            moved[t] = total * (1.0 / H2)
             move_copy(t).start()
 
+        from_planes(d4, fields_ref.at[0], range(own_tiles))
         for t in range(STEPS):
             floor_ref[0, t] = dense(arrived[t, 0:8], 1)
             move_copy(t).wait_send()
@@ -510,7 +496,11 @@
     groups = own_tiles // PERIOD
     cells = own // PLANES
     field = pltpu.VMEM((ROWS, (own_tiles + 2 * PAD) * LANES), jnp.float32)
-    pattern = pltpu.VMEM((ROWS, PERIOD * LANES), jnp.float32)
+    planes = pltpu.VMEM((SLOTS, 3, ROWS, LANES), jnp.float32)
+
+    def per_level(count):
+        return pltpu.VMEM((STEPS, SLOTS) + count + (ROWS, LANES), jnp.float32)
+
     anywhere = pl.BlockSpec(memory_space=pl.ANY)
     near = pl.BlockSpec(memory_space=pltpu.VMEM)
     dma = pltpu.SemaphoreType.DMA
@@ -522,17 +512,15 @@
         ),
         in_specs=[anywhere] * 4,
         out_specs=(near, near),
-        scratch_shapes=[field] * 8
+        scratch_shapes=[field] * 6
+        + [planes] * 7
+        + [per_level((2,)), per_level((2,)), per_level(()), per_level(()), per_level((3,))]
         + [
-            pltpu.VMEM((ROWS, PERIOD * LANES), jnp.int32),
-            pattern,
-            pattern,
             pltpu.VMEM(prior.shape, jnp.float32),
             pltpu.VMEM((len(DIRS), STEPS - 1) + prior.shape[1:], jnp.float32),
             pltpu.VMEM((STEPS, ROWS, LANES), jnp.float32),
             pltpu.VMEM((STEPS, ROWS, LANES), jnp.float32),
             pltpu.VMEM((STEPS, ROWS, (groups + 2) * LANES), jnp.float32),
-            pltpu.VMEM((8, groups * LANES), jnp.float32),
             pltpu.VMEM((STEPS, 8, LANES), jnp.float32),
             pltpu.VMEM((STEPS, 8, LANES), jnp.float32),
             dma((4,)),

time: 34.5 us -> 26.9 us (0.78)
  Pallas kernels: 31.5 us -> 23.9 us
    pallas_call x1, Pallas kernels: 31.5 us -> 23.9 us  [on_device(): pl.pallas_call(functools.partial(kernel, sizes, own_tiles), out_shape=(ja...]
where the time goes in v2:
time: 26.9 us; the launch traced here: 26.8 us
  Pallas kernels  23.9 us (89%)
  local copies, waits for them, and re-layouts  2.2 us (8%)
  between operations  0.65 us (2%)
    pallas_call x1, Pallas kernels, on_device(): pl.pallas_call(functools.partial(kernel, sizes, own_tiles), out_shape=(ja...  23.9 us
    unnamed x4, local copies, waits for them, and re-layouts  2.2 us

profile of v2, /device:TPU:216, one launch (start us, length us, event | category | flops | bytes accessed | tf_op | source)
XLA Modules:
  0.0 26.8 jit_solution(15074908103290392896)
XLA Ops:
  0.6 23.9 %shard_map.59 = (f32[1,8,4608]{2,1,0:T(8,128)}, f32[1,4,8,32]{3,2,1,0:T(8,128)}) custom-call(f32[1,8,4608]{2,1,0:T(8,128)} %cur_hbm.1, f32[1,8,4608]{2,1,0:T(8,128)} %prev_hbm.1, f32[1,8,4608]{2,1,0:T(8,128)} %mat_hbm.1, f32[4,8,32]{2,1,0:T(8,128)} %prior_hbm.1), custom_call_target="tpu_custom_call" | custom-call | tf_op jit(solution)/shard_map/pallas_call | solution.py:507
  24.6 0.0 copy-start
  24.6 1.6 %copy.8 = f32[1,8,4608]{2,1,0:T(8,128)} copy(f32[1,8,4608]{2,1,0:T(8,128)} %get-tuple-element.4) | data formatting | bytes 294912
  26.2 0.0 copy-done
  26.2 0.6 %copy.9 = f32[1,4,8,32]{3,2,1,0:T(8,128)} copy(f32[1,4,8,32]{3,2,1,0:T(8,128)S(1)} %copy-done) | data formatting | bytes 8192
Async XLA Ops:
  24.6 1.6 %copy-start = (f32[1,4,8,32]{3,2,1,0:T(8,128)S(1)}, f32[1,4,8,32]{3,2,1,0:T(8,128)}, u32[]{:S(2)}) copy-start(f32[1,4,8,32]{3,2,1,0:T(8,128)} %get-tuple-element.5) | copy-start | bytes 12292

commit v3 on v2

--- a/solution.py
+++ b/solution.py
@@ -17,7 +17,6 @@
 LANES = 128
 ROWS = 16
 PAD = 8
-SPAN = 2
 HALVES = 16
 SLOTS = HALVES + 2 * STEPS
 PERIOD = 9
@@ -32,12 +31,12 @@
     return pl.ds(start, count * LANES)
 
 
-def rows_sent(dx):
-    return {0: pl.ds(0, 8), 1: pl.ds(4, 4), -1: pl.ds(0, 4)}[dx]
-
-
-def rows_landed(dx):
-    return {0: pl.ds(0, 8), 1: pl.ds(12, 4), -1: pl.ds(8, 4)}[dx]
+def rows_sent(dx, depth):
+    return {0: pl.ds(0, 8), 1: pl.ds(8 - depth, depth), -1: pl.ds(0, depth)}[dx]
+
+
+def rows_landed(dx, depth):
+    return {0: pl.ds(0, 8), 1: pl.ds(16 - depth, depth), -1: pl.ds(8, depth)}[dx]
 
 
 def shift_x(value, by):
@@ -205,7 +204,7 @@
 def kernel(
     sizes, own_tiles, cur_hbm, prev_hbm, mat_hbm, prior_hbm, fields_ref, floor_ref,
     cur, prev, mat, p1, p2, p3, d0, d1, d2, d3, d4, before, stiff, sz, sx, ex, ez, lap,
-    prior, rims, packed, arrived, spread, moved, returned,
+    prior, outgoing, rims, packed, arrived, spread, moved, returned,
     load_sem, send_sem, recv_sem, prior_send, prior_recv, trace_send, trace_recv, move_send, move_recv,
 ):
     half, gx, gy = lax.axis_index("half"), lax.axis_index("gx"), lax.axis_index("gy")
@@ -239,7 +238,8 @@
 
     def halo_copies(dx, dy):
         out = []
-        for n, (ref, width) in enumerate(((cur, 5), (prev, 4), (mat, 4))):
+        for n, (ref, depth) in enumerate(((cur, STEPS), (prev, STEPS - 1), (mat, STEPS - 1))):
+            width = -(-depth * PLANES // LANES)
             if dy == 0:
                 src_lanes = dst_lanes = lanes_of(0, own_tiles)
             elif dy == 1:
@@ -249,8 +249,8 @@
             slot = DIRS.index((dx, dy)) * 3 + n
             out.append(
                 pltpu.make_async_remote_copy(
-                    src_ref=ref.at[rows_sent(dx), src_lanes],
-                    dst_ref=ref.at[rows_landed(dx), dst_lanes],
+                    src_ref=ref.at[rows_sent(dx, depth), src_lanes],
+                    dst_ref=ref.at[rows_landed(dx, depth), dst_lanes],
                     send_sem=send_sem.at[slot],
                     recv_sem=recv_sem.at[slot],
                     device_id={"gx": gx + dx, "gy": gy + dy},
@@ -262,8 +262,8 @@
     def prior_copy(dx, dy):
         slot = DIRS.index((dx, dy))
         return pltpu.make_async_remote_copy(
-            src_ref=prior.at[pl.ds(0, STEPS - 1)],
-            dst_ref=rims.at[slot],
+            src_ref=outgoing.at[rows_sent(dx, STEPS)],
+            dst_ref=rims.at[slot, rows_landed(dx, STEPS) if dx == 0 else rows_sent(dx, STEPS)],
             send_sem=prior_send.at[slot],
             recv_sem=prior_recv.at[slot],
             device_id={"gx": gx + dx, "gy": gy + dy},
@@ -275,11 +275,14 @@
         def _(dx=dx, dy=dy):
             lanes = {0: lanes_of(0, own_tiles), 1: lanes_of(-5, 5), -1: lanes_of(own_tiles, 5)}[dy]
             for ref in (cur, prev, mat):
-                ref[rows_landed(dx), lanes] = jnp.zeros((8 if dx == 0 else 4, lanes.size), jnp.float32)
+                ref[rows_landed(dx, STEPS), lanes] = jnp.zeros((8 if dx == 0 else 4, lanes.size), jnp.float32)
             rims[DIRS.index((dx, dy))] = jnp.zeros(rims.shape[1:], jnp.float32)
 
     for copy in loads:
         copy.wait()
+    cells = prior.shape[2]
+    idle = jnp.zeros((8, LANES - (STEPS - 1) * cells), jnp.float32)
+    outgoing[...] = jnp.concatenate([prior[t] for t in range(STEPS - 1)] + [idle], 1)
     pl.semaphore_wait(barrier, count)
 
     order = sorted(DIRS, key=lambda d: (d[1] == 0, d[0] != 0))
@@ -293,9 +296,9 @@
             def _():
                 prior_copy(dx, dy).start()
 
-    for dx, dy in DIRS:
+    def await_rim(dx, dy):
         @pl.when(exists(-dx, -dy))
-        def _(dx=dx, dy=dy):
+        def _():
             for copy in halo_copies(dx, dy):
                 copy.wait_recv()
 
@@ -309,16 +312,8 @@
     width = own_tiles * LANES
 
     def over_tiles(block, t):
-        margin = STEPS - 1 - t
-        edge = -(-margin * PLANES // LANES)
-        if edge:
-            block(0, range(-edge, 0), 0)
-        @pl.loop(0, groups)
-        def _(g):
-            block(g * PERIOD, range(PERIOD), g + 1)
-
-        if edge:
-            block(own_tiles, range(edge), groups + 1)
+        edge = -(-(STEPS - 1 - t) * PLANES // LANES)
+        block(range(-edge, own_tiles + edge))
 
     def trace_copy(t):
         return pltpu.make_async_remote_copy(
@@ -341,67 +336,90 @@
 
     @pl.when(wet)
     def _():
-        cells = 8 * groups
+        for dx, dy in DIRS:
+            await_rim(dx, dy)
+
+        sixteenth = lane // 16
+        blocks = range(-1, groups + 1)
+
+        def deepest(ref, reach):
+            tiles = {}
+            for g in blocks:
+                tile = None
+                for j in range(8):
+                    q = g * PERIOD + j + 1
+                    if -STEPS <= q <= own_tiles + reach:
+                        value = ref[:, lanes_of(q)]
+                        tile = value if tile is None else jnp.where(sixteenth == j, value, tile)
+                tiles[g] = tile
+            return tiles
+
+        floor_lanes = lane % 16 == 15
+
+        def send_trace(t, tiles):
+            total = None
+            for g in blocks:
+                tile = turn(jnp.where(floor_lanes, tiles[g], 0.0), 15 - (g + 1))
+                total = tile if total is None else total + tile
+            packed[t] = total
+            trace_copy(t).start()
+
+        now, then = deepest(cur, STEPS), deepest(prev, STEPS - 1)
+        send_trace(0, now)
+
         row = lax.broadcasted_iota(jnp.int32, (cells, groups * LANES), 0)
         col = lax.broadcasted_iota(jnp.int32, (cells, groups * LANES), 1)
         place = (col == LANES * (row // 8) + 16 * (row % 8) + 15).astype(jnp.float32)
         upper = lax.broadcasted_iota(jnp.int32, (8, cells), 0) < 4
 
         def rim(dx, dy, t):
-            return rims[DIRS.index((dx, dy)), t]
-
-        for t in range(STEPS):
-            centre = prior[t]
-            if t == STEPS - 1:
-                spread[t, 0:8, pl.ds(LANES, groups * LANES)] = exact_dot(centre, place)
-                continue
-            for dy, value in (
-                (0, jnp.concatenate([centre, jnp.where(upper, rim(-1, 0, t), rim(1, 0, t))], 0)),
-                (1, jnp.concatenate([rim(0, 1, t), jnp.where(upper, rim(-1, 1, t), rim(1, 1, t))], 0)),
-                (-1, jnp.concatenate([rim(0, -1, t), jnp.where(upper, rim(-1, -1, t), rim(1, -1, t))], 0)),
-            ):
-                if dy == 0:
-                    spread[t, :, pl.ds(LANES, groups * LANES)] = exact_dot(value, place)
-                elif dy == 1:
-                    spread[t, :, pl.ds(0, LANES)] = exact_dot(value, place[:, (groups - 1) * LANES:])
-                else:
-                    spread[t, :, pl.ds((groups + 1) * LANES, LANES)] = exact_dot(value, place[:, :LANES])
+            return (outgoing[...] if dx == dy == 0 else rims[DIRS.index((dx, dy))])[:, t * cells : (t + 1) * cells]
+
+        for dy, first, count in ((0, 0, groups), (1, groups - 1, 1), (-1, 0, 1)):
+            rows = []
+            for t in range(STEPS - 1):
+                rows += [rim(0, dy, t), jnp.where(upper, rim(-1, dy, t), rim(1, dy, t))]
+            value = exact_dot(jnp.concatenate(rows, 0), place[:, first * LANES : (first + count) * LANES])
+            at = {0: 1, 1: 0, -1: groups + 1}[dy]
+            for t in range(STEPS - 1):
+                spread[t, :, pl.ds(at * LANES, count * LANES)] = value[t * ROWS : (t + 1) * ROWS]
+
+        def ghost_tile(t, g):
+            return spread[t, :, pl.ds((g + 1) * LANES, LANES)]
+
+        speed = deepest(mat, STEPS - 1)
+        for t in range(STEPS - 1):
+            memo = Tiles()
+            later = {}
+            inside = {g: now[g] for g in blocks}
+            inside[-2] = inside[groups + 1] = jnp.zeros((ROWS, LANES), jnp.float32)
+
+            def of(g, inside=inside):
+                return inside[g]
+
+            for g in blocks:
+                u = now[g]
+                below = jnp.where(floor_lanes, u - ghost_tile(t, g), turn(u, 1))
+                total = (shift_x(u, 1) + shift_x(u, -1)) + (below + turn(u, -1))
+                total = total + (
+                    flat_shift(memo, "u", of, lane, g, 16) + flat_shift(memo, "u", of, lane, g, -16)
+                )
+                later[g] = (u + u) - then[g] + (H2 * speed[g]) * (total - 6.0 * u)
+            then, now = now, later
+            send_trace(t + 1, now)
+
+        spread[STEPS - 1, 0:8, pl.ds(LANES, groups * LANES)] = exact_dot(prior[STEPS - 1], place)
 
         for t in range(STEPS):
             src, old = levels[t], olds[t]
-            margin = STEPS - 1 - t
-            total = None
-            for g in range(-1, groups + 1):
-                tile = None
-                for j in range(8):
-                    q = g * PERIOD + j + 1
-                    edge = -(-margin * PLANES // LANES)
-                    if q < -edge or q >= own_tiles + edge:
-                        continue
-                    value = src[:, lanes_of(q)]
-                    tile = value if tile is None else jnp.where(lane == 16 * j + 15, value, tile)
-                if tile is None:
-                    continue
-                tile = jnp.where(lane % 16 == 15, tile, 0.0)
-                tile = turn(tile, 15 - (g + 1))
-                total = tile if total is None else total + tile
-            packed[t] = total
-            trace_copy(t).start()
-
-            def block(base, tiles, slot, t=t, src=src, old=old):
-                last = t == STEPS - 1
-                start = 0
-                if last:
-                    start = pl.multiple_of(base * LANES, LANES)
-
+            last = t == STEPS - 1
+
+            def block(tiles, t=t, src=src, old=old, last=last):
                 def ghost(j):
-                    at = slot * LANES
-                    if not isinstance(at, int):
-                        at = pl.multiple_of(at, LANES)
-                    return spread[t, :, pl.ds(at, LANES)]
+                    return ghost_tile(t, (j - 1) // PERIOD)
 
                 dst = fields_ref.at[0] if last else levels[t + 1]
-                water_block(src, old, dst, mat, ghost, start, base, tiles, last)
+                water_block(src, old, dst, mat, ghost, 0, 0, tiles, last)
 
             over_tiles(block, t)
 
@@ -431,11 +449,21 @@
             to_planes(prev, rows, inner, base, put(before))
             to_planes(mat, rows, inner, base, put_stiff)
 
-        for rows in (pl.ds(0, 8), pl.ds(8, 8)):
+        def convert_inner(rows):
             @pl.loop(0, HALVES // 8)
-            def _(n, rows=rows):
+            def _(n):
                 convert(rows, range(STEPS, STEPS + 8), n * PERIOD, n * 8)
 
+        upper, lower = pl.ds(0, 8), pl.ds(8, 8)
+        convert_inner(upper)
+        for dx, dy in DIRS:
+            if dy == 0:
+                await_rim(dx, dy)
+        convert_inner(lower)
+        for dx, dy in DIRS:
+            if dy != 0:
+                await_rim(dx, dy)
+        for rows in (upper, lower):
             convert(rows, (*range(STEPS), *range(SLOTS - STEPS, SLOTS)))
 
         displaced = (d0, d1, d2, d3, d4)
@@ -448,10 +476,8 @@
             rows = 8 if last else ROWS
             src, old, dst = displaced[t], earlier[t], displaced[t + 1]
 
-            @pl.loop(t, SLOTS - t, step=SPAN)
-            def _(first, t=t, src=src, rows=rows):
-                for k in range(SPAN):
-                    slopes(src, t, first + k, *scratch, rows)
+            for slot in range(t, SLOTS - t):
+                slopes(src, t, slot, *scratch, rows)
 
             trace_copy(t).wait_recv()
             load = arrived[t][:rows]
@@ -490,6 +516,17 @@
                 prior_copy(dx, dy).wait_send()
 
 
+def deliver(fields_ref, floor_ref, fields_out, floor_out, sem):
+    copies = [
+        pltpu.make_async_copy(src, dst, sem.at[n])
+        for n, (src, dst) in enumerate(((fields_ref, fields_out), (floor_ref, floor_out)))
+    ]
+    for copy in copies:
+        copy.start()
+    for copy in copies:
+        copy.wait()
+
+
 def on_device(sizes, current, previous, material, prior):
     own = current.shape[2]
     own_tiles = own // LANES
@@ -504,11 +541,11 @@
     anywhere = pl.BlockSpec(memory_space=pl.ANY)
     near = pl.BlockSpec(memory_space=pltpu.VMEM)
     dma = pltpu.SemaphoreType.DMA
-    return pl.pallas_call(
+    held = pl.pallas_call(
         functools.partial(kernel, sizes, own_tiles),
         out_shape=(
-            jax.ShapeDtypeStruct(current.shape, jnp.float32),
-            jax.ShapeDtypeStruct((1,) + prior.shape, jnp.float32),
+            pltpu.VMEM(current.shape, jnp.float32),
+            pltpu.VMEM((1,) + prior.shape, jnp.float32),
         ),
         in_specs=[anywhere] * 4,
         out_specs=(near, near),
@@ -517,7 +554,8 @@
         + [per_level((2,)), per_level((2,)), per_level(()), per_level(()), per_level((3,))]
         + [
             pltpu.VMEM(prior.shape, jnp.float32),
-            pltpu.VMEM((len(DIRS), STEPS - 1) + prior.shape[1:], jnp.float32),
+            pltpu.VMEM((8, LANES), jnp.float32),
+            pltpu.VMEM((len(DIRS), 8, LANES), jnp.float32),
             pltpu.VMEM((STEPS, ROWS, LANES), jnp.float32),
             pltpu.VMEM((STEPS, ROWS, LANES), jnp.float32),
             pltpu.VMEM((STEPS, ROWS, (groups + 2) * LANES), jnp.float32),
@@ -535,6 +573,13 @@
         ],
         compiler_params=pltpu.CompilerParams(collective_id=0, has_side_effects=True),
     )(current, previous, material, prior)
+    return pl.pallas_call(
+        deliver,
+        out_shape=tuple(jax.ShapeDtypeStruct(x.shape, x.dtype) for x in held),
+        in_specs=[near] * 2,
+        out_specs=(anywhere, anywhere),
+        scratch_shapes=[dma((2,))],
+    )(*(pltpu.with_memory_space_constraint(x, pltpu.VMEM) for x in held))
 
 
 def solution(mesh):

time: 26.9 us -> 21.4 us (0.80)
  Pallas kernels: 23.9 us -> 20.6 us
  local copies, waits for them, and re-layouts: 2.2 us -> 0 us
    pallas_call x1 -> x2, Pallas kernels: 23.9 us -> 20.6 us  [the longest x1 19.9 us: on_device(): pl.pallas_call(functools.partial(kernel, sizes, own_tiles), out_shape=(pl...]
    unnamed x4 -> x0, local copies, waits for them, and re-layouts: 2.2 us -> none
where the time goes in v3:
time: 21.4 us; the launch traced here: 21.3 us
  Pallas kernels  20.6 us (96%)
  between operations  0.64 us (3%)
    pallas_call x1, Pallas kernels, on_device(): pl.pallas_call(functools.partial(kernel, sizes, own_tiles), out_shape=(pl...  19.9 us
    pallas_call x1, Pallas kernels, on_device(): pl.pallas_call(deliver, out_shape=tuple((jax.ShapeDtypeStruct(x.shape, x....  0.68 us

profile of v3, /device:TPU:216, one launch (start us, length us, event | category | flops | bytes accessed | tf_op | source)
XLA Modules:
  0.0 21.3 jit_solution(10666233852559770101)
XLA Ops:
  0.6 19.9 %shard_map.59 = (f32[1,8,4608]{2,1,0:T(8,128)S(1)}, f32[1,4,8,32]{3,2,1,0:T(8,128)S(1)}) custom-call(f32[1,8,4608]{2,1,0:T(8,128)} %cur_hbm.1, f32[1,8,4608]{2,1,0:T(8,128)} %prev_hbm.1, f32[1,8,4608]{2,1,0:T(8,128)} %mat_hbm.1, f32[4,8,32]{2,1,0:T(8,128)} %prior_hbm.1), custom_call_target="tpu_custom_call" | custom-call | tf_op jit(solution)/shard_map/pallas_call | solution.py:544
  20.6 0.7 %shard_map.60 = (f32[1,8,4608]{2,1,0:T(8,128)}, f32[1,4,8,32]{3,2,1,0:T(8,128)}) custom-call(f32[1,8,4608]{2,1,0:T(8,128)S(1)} %get-tuple-element.4.fields_ref, f32[1,4,8,32]{3,2,1,0:T(8,128)S(1)} %get-tuple-element.5.floor_ref), custom_call_target="tpu_custom_call" | custom-call | tf_op jit(solution)/shard_map/pallas_call | solution.py:576

commit v4 on v3

--- a/solution.py
+++ b/solution.py
@@ -204,8 +204,8 @@
 def kernel(
     sizes, own_tiles, cur_hbm, prev_hbm, mat_hbm, prior_hbm, fields_ref, floor_ref,
     cur, prev, mat, p1, p2, p3, d0, d1, d2, d3, d4, before, stiff, sz, sx, ex, ez, lap,
-    prior, outgoing, rims, packed, arrived, spread, moved, returned,
-    load_sem, send_sem, recv_sem, prior_send, prior_recv, trace_send, trace_recv, move_send, move_recv,
+    prior, deep, packed, arrived, spread, moved, returned,
+    load_sem, send_sem, recv_sem, deep_send, deep_recv, trace_send, trace_recv, move_send, move_recv,
 ):
     half, gx, gy = lax.axis_index("half"), lax.axis_index("gx"), lax.axis_index("gy")
     n_x, n_y = sizes
@@ -259,13 +259,20 @@
             )
         return out
 
-    def prior_copy(dx, dy):
+    def deep_lanes(dy, landed):
+        if dy == 0:
+            return pl.ds(LANES, groups * LANES)
+        if landed:
+            return pl.ds(0 if dy == 1 else (groups + 1) * LANES, LANES)
+        return pl.ds((groups if dy == 1 else 1) * LANES, LANES)
+
+    def deep_copy(dx, dy):
         slot = DIRS.index((dx, dy))
         return pltpu.make_async_remote_copy(
-            src_ref=outgoing.at[rows_sent(dx, STEPS)],
-            dst_ref=rims.at[slot, rows_landed(dx, STEPS) if dx == 0 else rows_sent(dx, STEPS)],
-            send_sem=prior_send.at[slot],
-            recv_sem=prior_recv.at[slot],
+            src_ref=deep.at[rows_sent(dx, STEPS), deep_lanes(dy, False)],
+            dst_ref=deep.at[rows_landed(dx, STEPS), deep_lanes(dy, True)],
+            send_sem=deep_send.at[slot],
+            recv_sem=deep_recv.at[slot],
             device_id={"gx": gx + dx, "gy": gy + dy},
             device_id_type=MESH,
         )
@@ -276,37 +283,56 @@
             lanes = {0: lanes_of(0, own_tiles), 1: lanes_of(-5, 5), -1: lanes_of(own_tiles, 5)}[dy]
             for ref in (cur, prev, mat):
                 ref[rows_landed(dx, STEPS), lanes] = jnp.zeros((8 if dx == 0 else 4, lanes.size), jnp.float32)
-            rims[DIRS.index((dx, dy))] = jnp.zeros(rims.shape[1:], jnp.float32)
+            lanes = deep_lanes(dy, True)
+            deep[rows_landed(dx, STEPS), lanes] = jnp.zeros((8 if dx == 0 else STEPS, lanes.size), jnp.float32)
 
     for copy in loads:
         copy.wait()
-    cells = prior.shape[2]
-    idle = jnp.zeros((8, LANES - (STEPS - 1) * cells), jnp.float32)
-    outgoing[...] = jnp.concatenate([prior[t] for t in range(STEPS - 1)] + [idle], 1)
+    lane = lax.broadcasted_iota(jnp.int32, (ROWS, LANES), 1)
+    lane8 = lane[:8]
+    within = lane8 % 16
+
+    @pl.when(wet)
+    def _():
+        cells = 8 * groups
+        row = lax.broadcasted_iota(jnp.int32, (cells, groups * LANES), 0)
+        col = lax.broadcasted_iota(jnp.int32, (cells, groups * LANES), 1)
+        place = (col == LANES * (row // 8) + 16 * (row % 8) + 15).astype(jnp.float32)
+        wave = exact_dot(jnp.concatenate([prior[t] for t in range(STEPS)], 0), place)
+        spread[STEPS - 1, 0:8, pl.ds(LANES, groups * LANES)] = wave[8 * (STEPS - 1) :]
+
+        for g in range(groups):
+            tile = jnp.zeros((8, LANES), jnp.float32)
+            for n, (ref, depth) in enumerate(((cur, STEPS), (prev, STEPS - 1), (mat, STEPS - 1))):
+                planes = None
+                for j in range(8):
+                    value = ref[0:8, lanes_of(g * PERIOD + j + 1)]
+                    planes = value if planes is None else jnp.where(lane8 // 16 == j, value, planes)
+                tile = tile + turn(jnp.where(within >= 16 - depth, planes, 0.0), 4 * n)
+            for t in range(STEPS - 1):
+                tile = tile + turn(wave[8 * t : 8 * t + 8, g * LANES : (g + 1) * LANES], 15 - t)
+            deep[0:8, pl.ds((g + 1) * LANES, LANES)] = tile
+
     pl.semaphore_wait(barrier, count)
 
     order = sorted(DIRS, key=lambda d: (d[1] == 0, d[0] != 0))
+    for dx, dy in order:
+        @pl.when(exists(dx, dy) & wet)
+        def _(dx=dx, dy=dy):
+            deep_copy(dx, dy).start()
+
     for dx, dy in order:
         @pl.when(exists(dx, dy))
         def _(dx=dx, dy=dy):
             for copy in halo_copies(dx, dy):
                 copy.start()
 
-            @pl.when(wet)
-            def _():
-                prior_copy(dx, dy).start()
-
     def await_rim(dx, dy):
         @pl.when(exists(-dx, -dy))
         def _():
             for copy in halo_copies(dx, dy):
                 copy.wait_recv()
 
-            @pl.when(wet)
-            def _():
-                prior_copy(dx, dy).wait_recv()
-
-    lane = lax.broadcasted_iota(jnp.int32, (ROWS, LANES), 1)
     levels = (cur, p1, p2, p3)
     olds = (prev, cur, p1, p2)
     width = own_tiles * LANES
@@ -337,23 +363,11 @@
     @pl.when(wet)
     def _():
         for dx, dy in DIRS:
-            await_rim(dx, dy)
-
-        sixteenth = lane // 16
+            @pl.when(exists(-dx, -dy))
+            def _(dx=dx, dy=dy):
+                deep_copy(dx, dy).wait_recv()
+
         blocks = range(-1, groups + 1)
-
-        def deepest(ref, reach):
-            tiles = {}
-            for g in blocks:
-                tile = None
-                for j in range(8):
-                    q = g * PERIOD + j + 1
-                    if -STEPS <= q <= own_tiles + reach:
-                        value = ref[:, lanes_of(q)]
-                        tile = value if tile is None else jnp.where(sixteenth == j, value, tile)
-                tiles[g] = tile
-            return tiles
-
         floor_lanes = lane % 16 == 15
 
         def send_trace(t, tiles):
@@ -364,30 +378,16 @@
             packed[t] = total
             trace_copy(t).start()
 
-        now, then = deepest(cur, STEPS), deepest(prev, STEPS - 1)
-        send_trace(0, now)
-
-        row = lax.broadcasted_iota(jnp.int32, (cells, groups * LANES), 0)
-        col = lax.broadcasted_iota(jnp.int32, (cells, groups * LANES), 1)
-        place = (col == LANES * (row // 8) + 16 * (row % 8) + 15).astype(jnp.float32)
-        upper = lax.broadcasted_iota(jnp.int32, (8, cells), 0) < 4
-
-        def rim(dx, dy, t):
-            return (outgoing[...] if dx == dy == 0 else rims[DIRS.index((dx, dy))])[:, t * cells : (t + 1) * cells]
-
-        for dy, first, count in ((0, 0, groups), (1, groups - 1, 1), (-1, 0, 1)):
-            rows = []
-            for t in range(STEPS - 1):
-                rows += [rim(0, dy, t), jnp.where(upper, rim(-1, dy, t), rim(1, dy, t))]
-            value = exact_dot(jnp.concatenate(rows, 0), place[:, first * LANES : (first + count) * LANES])
-            at = {0: 1, 1: 0, -1: groups + 1}[dy]
-            for t in range(STEPS - 1):
-                spread[t, :, pl.ds(at * LANES, count * LANES)] = value[t * ROWS : (t + 1) * ROWS]
-
         def ghost_tile(t, g):
             return spread[t, :, pl.ds((g + 1) * LANES, LANES)]
 
-        speed = deepest(mat, STEPS - 1)
+        now = {g: deep[:, pl.ds((g + 1) * LANES, LANES)] for g in blocks}
+        send_trace(0, now)
+        then = {g: turn(now[g], -4) for g in blocks}
+        speed = {g: turn(now[g], -8) for g in blocks}
+        for t in range(STEPS - 1):
+            for g in blocks:
+                spread[t, :, pl.ds((g + 1) * LANES, LANES)] = turn(now[g], t - 15)
         for t in range(STEPS - 1):
             memo = Tiles()
             later = {}
@@ -408,7 +408,8 @@
             then, now = now, later
             send_trace(t + 1, now)
 
-        spread[STEPS - 1, 0:8, pl.ds(LANES, groups * LANES)] = exact_dot(prior[STEPS - 1], place)
+        for dx, dy in DIRS:
+            await_rim(dx, dy)
 
         for t in range(STEPS):
             src, old = levels[t], olds[t]
@@ -469,8 +470,6 @@
         displaced = (d0, d1, d2, d3, d4)
         earlier = (before, d0, d1, d2)
         scratch = (sz, sx, ex, ez, lap)
-        lane8 = lane[:8]
-
         for t in range(STEPS):
             last = t == STEPS - 1
             rows = 8 if last else ROWS
@@ -513,7 +512,7 @@
 
             @pl.when(wet)
             def _():
-                prior_copy(dx, dy).wait_send()
+                deep_copy(dx, dy).wait_send()
 
 
 def deliver(fields_ref, floor_ref, fields_out, floor_out, sem):
@@ -554,8 +553,7 @@
         + [per_level((2,)), per_level((2,)), per_level(()), per_level(()), per_level((3,))]
         + [
             pltpu.VMEM(prior.shape, jnp.float32),
-            pltpu.VMEM((8, LANES), jnp.float32),
-            pltpu.VMEM((len(DIRS), 8, LANES), jnp.float32),
+            pltpu.VMEM((ROWS, (groups + 2) * LANES), jnp.float32),
             pltpu.VMEM((STEPS, ROWS, LANES), jnp.float32),
             pltpu.VMEM((STEPS, ROWS, LANES), jnp.float32),
             pltpu.VMEM((STEPS, ROWS, (groups + 2) * LANES), jnp.float32),

time: 21.4 us -> 20.2 us (0.944)
  Pallas kernels: 20.6 us -> 19.5 us
    pallas_call x1, Pallas kernels: 19.9 us -> 18.8 us  [on_device(): pl.pallas_call(functools.partial(kernel, sizes, own_tiles), out_shape=(pl...]
where the time goes in v4:
time: 20.2 us; the launch traced here: 20.1 us
  Pallas kernels  19.5 us (97%)
  between operations  0.64 us (3%)
    pallas_call x1, Pallas kernels, on_device(): pl.pallas_call(functools.partial(kernel, sizes, own_tiles), out_shape=(pl...  18.8 us
    pallas_call x1, Pallas kernels, on_device(): pl.pallas_call(deliver, out_shape=tuple((jax.ShapeDtypeStruct(x.shape, x....  0.68 us

profile of v4, /device:TPU:216, one launch (start us, length us, event | category | flops | bytes accessed | tf_op | source)
XLA Modules:
  0.0 20.1 jit_solution(5435325537497702173)
XLA Ops:
  0.6 18.8 %shard_map.59 = (f32[1,8,4608]{2,1,0:T(8,128)S(1)}, f32[1,4,8,32]{3,2,1,0:T(8,128)S(1)}) custom-call(f32[1,8,4608]{2,1,0:T(8,128)} %cur_hbm.1, f32[1,8,4608]{2,1,0:T(8,128)} %prev_hbm.1, f32[1,8,4608]{2,1,0:T(8,128)} %mat_hbm.1, f32[4,8,32]{2,1,0:T(8,128)} %prior_hbm.1), custom_call_target="tpu_custom_call" | custom-call | tf_op jit(solution)/shard_map/pallas_call | solution.py:543
  19.4 0.7 %shard_map.60 = (f32[1,8,4608]{2,1,0:T(8,128)}, f32[1,4,8,32]{3,2,1,0:T(8,128)}) custom-call(f32[1,8,4608]{2,1,0:T(8,128)S(1)} %get-tuple-element.4.fields_ref, f32[1,4,8,32]{3,2,1,0:T(8,128)S(1)} %get-tuple-element.5.floor_ref), custom_call_target="tpu_custom_call" | custom-call | tf_op jit(solution)/shard_map/pallas_call | solution.py:574

commit v5 on v4

--- a/solution.py
+++ b/solution.py
@@ -191,6 +191,54 @@
             dst[:, lanes_of(base + j)] = new
 
 
+def top_slopes(src, c, g, at, sz, sx, ex, lap, rows):
+    lane = lax.broadcasted_iota(jnp.int32, (ROWS, LANES), 1)
+    u = src[c, :, at(g)]
+    up, down = turn(u, 1), jnp.where(lane % 16 == 0, 0.0, turn(u, -1))
+    right, left = shift_x(u, 1)[:rows], shift_x(u, -1)[:rows]
+    slope = (up - down) * 0.25
+    sz[c, 0:rows, at(g)] = slope[:rows]
+    sx[c, 0:rows, at(g)] = (right - left) * 0.25
+    lap_x, lap_z = right + left, (up + down)[:rows]
+    lap[c, 0:rows, at(g)] = lap_x + lap_z
+    mixed = (shift_x(slope, 1) - shift_x(slope, -1))[:rows]
+    ex[c, 0:rows, at(g)] = mixed
+    return lap_x, lap_z
+
+
+def top_update(src, old, dst, g, at, sz, sx, ex, self_terms, lap, stiff, pushed, rows):
+    lane = lax.broadcasted_iota(jnp.int32, (rows, LANES), 1)
+    memo = Tiles()
+
+    def along(name, ref, c, by):
+        return flat_shift(memo, (name, c), lambda n: ref[c, 0:rows, at(n)], lane, g, by)
+
+    def cross(name, ref, c):
+        return along(name, ref, c, 16) - along(name, ref, c, -16)
+
+    bulk, shear, light = (stiff[n, 0:rows, at(g)] for n in range(3))
+    acc = None
+    for c in range(3):
+        if dst is None and c < 2:
+            continue
+        u = src[c, 0:rows, at(g)]
+        lap_y = along("u", src, c, 16) + along("u", src, c, -16)
+        if c == 0:
+            grad = self_terms[0, 0:rows, at(g)] + (cross("sx", sx, 1) + ex[2, 0:rows, at(g)])
+        elif c == 1:
+            grad = lap_y + (cross("sx", sx, 0) + cross("sz", sz, 2))
+        else:
+            grad = self_terms[1, 0:rows, at(g)] + (ex[0, 0:rows, at(g)] + cross("sz", sz, 1))
+        twice = u + u
+        total = lap[c, 0:rows, at(g)] + lap_y - 6.0 * u
+        acc = bulk * (grad - twice) + shear * total
+        if c == 2:
+            acc = acc + light * pushed
+        if dst is not None:
+            dst[c, 0:rows, at(g)] = twice - old[c, 0:rows, at(g)] + acc
+    return acc
+
+
 def floor_lane(tile):
     if tile % PERIOD == 0:
         return None
@@ -204,8 +252,8 @@
 def kernel(
     sizes, own_tiles, cur_hbm, prev_hbm, mat_hbm, prior_hbm, fields_ref, floor_ref,
     cur, prev, mat, p1, p2, p3, d0, d1, d2, d3, d4, before, stiff, sz, sx, ex, ez, lap,
-    prior, deep, packed, arrived, spread, moved, returned,
-    load_sem, send_sem, recv_sem, deep_send, deep_recv, trace_send, trace_recv, move_send, move_recv,
+    prior, deep, packed, arrived, spread, crown, samples, t0, t1, t2, t3, told, tstiff, tsz, tsx, tex, tself, tlap,
+    load_sem, send_sem, recv_sem, deep_send, deep_recv, trace_send, trace_recv, crown_send, crown_recv,
 ):
     half, gx, gy = lax.axis_index("half"), lax.axis_index("gx"), lax.axis_index("gy")
     n_x, n_y = sizes
@@ -228,11 +276,13 @@
     count = jnp.int32(1)
     for dx, dy in DIRS:
         here = exists(dx, dy)
-        count = count + here.astype(jnp.int32)
+        count = count + 2 * here.astype(jnp.int32)
 
         @pl.when(here)
         def _(dx=dx, dy=dy):
-            pl.semaphore_signal(barrier, inc=1, device_id={"gx": gx + dx, "gy": gy + dy}, device_id_type=MESH)
+            for medium in (half, 1 - half):
+                there = {"half": medium, "gx": gx + dx, "gy": gy + dy}
+                pl.semaphore_signal(barrier, inc=1, device_id=there, device_id_type=MESH)
 
     pl.semaphore_signal(barrier, inc=1, device_id={"half": 1 - half}, device_id_type=MESH)
 
@@ -277,6 +327,24 @@
             device_id_type=MESH,
         )
 
+    def crown_copy(dx, dy):
+        slot = DIRS.index((dx, dy))
+        return pltpu.make_async_remote_copy(
+            src_ref=crown.at[:, rows_sent(dx, STEPS), deep_lanes(dy, False)],
+            dst_ref=crown.at[:, rows_landed(dx, STEPS), deep_lanes(dy, True)],
+            send_sem=crown_send.at[slot],
+            recv_sem=crown_recv.at[slot],
+            device_id={"half": 1 - half, "gx": gx + dx, "gy": gy + dy},
+            device_id_type=MESH,
+        )
+
+    def crown_up():
+        own = crown.at[:, 0:8, deep_lanes(0, False)]
+        return pltpu.make_async_remote_copy(
+            src_ref=own, dst_ref=own, send_sem=crown_send.at[len(DIRS)], recv_sem=crown_recv.at[len(DIRS)],
+            device_id={"half": 1 - half}, device_id_type=MESH,
+        )
+
     for dx, dy in DIRS:
         @pl.when(jnp.logical_not(exists(-dx, -dy)))
         def _(dx=dx, dy=dy):
@@ -284,7 +352,10 @@
             for ref in (cur, prev, mat):
                 ref[rows_landed(dx, STEPS), lanes] = jnp.zeros((8 if dx == 0 else 4, lanes.size), jnp.float32)
             lanes = deep_lanes(dy, True)
-            deep[rows_landed(dx, STEPS), lanes] = jnp.zeros((8 if dx == 0 else STEPS, lanes.size), jnp.float32)
+            blank = jnp.zeros((8 if dx == 0 else STEPS, lanes.size), jnp.float32)
+            deep[rows_landed(dx, STEPS), lanes] = blank
+            for c in range(3):
+                crown[c, rows_landed(dx, STEPS), lanes] = blank
 
     for copy in loads:
         copy.wait()
@@ -313,7 +384,26 @@
                 tile = tile + turn(wave[8 * t : 8 * t + 8, g * LANES : (g + 1) * LANES], 15 - t)
             deep[0:8, pl.ds((g + 1) * LANES, LANES)] = tile
 
+    @pl.when(jnp.logical_not(wet))
+    def _():
+        for g in range(groups):
+            for c in range(3):
+                tile = None
+                for ref, depth, lead in ((cur, 5, 0), (prev, 4, 5), (mat, 4, 9)):
+                    planes = None
+                    for j in range(8):
+                        q = g * PERIOD + (PLANES * j + THICK * c) // LANES
+                        spot = (j + 3 * c) % 8
+                        value = ref[0:8, lanes_of(q)]
+                        planes = value if planes is None else jnp.where(lane8 // 16 == spot, value, planes)
+                    part = jnp.where(within < depth, planes, 0.0)
+                    if (THICK * c - lead) % LANES:
+                        part = turn(part, THICK * c - lead)
+                    tile = part if tile is None else tile + part
+                crown[c, 0:8, pl.ds((g + 1) * LANES, LANES)] = tile
+
     pl.semaphore_wait(barrier, count)
+
 
     order = sorted(DIRS, key=lambda d: (d[1] == 0, d[0] != 0))
     for dx, dy in order:
@@ -321,6 +411,14 @@
         def _(dx=dx, dy=dy):
             deep_copy(dx, dy).start()
 
+        @pl.when(exists(dx, dy) & jnp.logical_not(wet))
+        def _(dx=dx, dy=dy):
+            crown_copy(dx, dy).start()
+
+    @pl.when(jnp.logical_not(wet))
+    def _():
+        crown_up().start()
+
     for dx, dy in order:
         @pl.when(exists(dx, dy))
         def _(dx=dx, dy=dy):
@@ -344,12 +442,6 @@
     def trace_copy(t):
         return pltpu.make_async_remote_copy(
             src_ref=packed.at[t], dst_ref=arrived.at[t], send_sem=trace_send.at[t], recv_sem=trace_recv.at[t],
-            device_id={"half": 1 - half}, device_id_type=MESH,
-        )
-
-    def move_copy(t):
-        return pltpu.make_async_remote_copy(
-            src_ref=moved.at[t], dst_ref=returned.at[t], send_sem=move_send.at[t], recv_sem=move_recv.at[t],
             device_id={"half": 1 - half}, device_id_type=MESH,
         )
 
@@ -371,6 +463,8 @@
         floor_lanes = lane % 16 == 15
 
         def send_trace(t, tiles):
+            for g in blocks:
+                samples[t, :, pl.ds((g + 1) * LANES, LANES)] = jnp.where(lane % 16 == 0, turn(tiles[g], 15), 0.0)
             total = None
             for g in blocks:
                 tile = turn(jnp.where(floor_lanes, tiles[g], 0.0), 15 - (g + 1))
@@ -409,6 +503,51 @@
             send_trace(t + 1, now)
 
         for dx, dy in DIRS:
+            @pl.when(exists(-dx, -dy))
+            def _(dx=dx, dy=dy):
+                crown_copy(dx, dy).wait_recv()
+
+        crown_up().wait_recv()
+
+        def at(g):
+            return pl.ds((g + 2) * LANES, LANES)
+
+        first_lanes = lane % 16 == 0
+        for ref in (t0, t1, t2, t3, tsz, tsx):
+            for c in range(3):
+                for g in (-2, groups + 1):
+                    ref[c, :, at(g)] = jnp.zeros((ROWS, LANES), jnp.float32)
+        for g in blocks:
+            tiles = [crown[c, :, pl.ds((g + 1) * LANES, LANES)] for c in range(3)]
+            light = H2 * turn(tiles[2], 9)
+            tstiff[0, :, at(g)] = light * turn(tiles[0], 9)
+            tstiff[1, :, at(g)] = light * turn(tiles[1], 9)
+            tstiff[2, :, at(g)] = light
+            for c in range(3):
+                t0[c, :, at(g)] = tiles[c]
+                told[c, :, at(g)] = turn(tiles[c], 5)
+
+        tops, befores = (t0, t1, t2, t3, None), (told, t0, t1, t2)
+        for t in range(STEPS):
+            last = t == STEPS - 1
+            rows = 8 if last else ROWS
+            for g in blocks:
+                terms = [top_slopes(tops[t], c, g, at, tsz, tsx, tex, tlap, rows) for c in range(3)]
+                tself[0, 0:rows, at(g)] = terms[0][0]
+                tself[1, 0:rows, at(g)] = terms[2][1]
+            total = None
+            for g in range(groups) if last else blocks:
+                source = samples[t, 0:rows, pl.ds((g + 1) * LANES, LANES)]
+                acc = top_update(
+                    tops[t], befores[t], tops[t + 1], g, at, tsz, tsx, tex, tself, tlap, tstiff, source, rows
+                )
+                if 0 <= g < groups:
+                    tile = turn(jnp.where(within == 0, acc[:8], 0.0), -g)
+                    total = tile if total is None else total + tile
+            floor_ref[0, t] = (RELAXATION / H2) * dense(total, 0) + (1.0 - RELAXATION) * prior[t]
+            trace_copy(t).wait_send()
+
+        for dx, dy in DIRS:
             await_rim(dx, dy)
 
         for t in range(STEPS):
@@ -423,12 +562,6 @@
                 water_block(src, old, dst, mat, ghost, 0, 0, tiles, last)
 
             over_tiles(block, t)
-
-        for t in range(STEPS):
-            move_copy(t).wait_recv()
-            motion = jnp.where(lane[:8] < HALVES, returned[t], turn(returned[t], THICK - HALVES))
-            floor_ref[0, t] = RELAXATION * motion[:, : 8 * groups] + (1.0 - RELAXATION) * prior[t]
-            trace_copy(t).wait_send()
 
     @pl.when(jnp.logical_not(wet))
     def _():
@@ -490,19 +623,13 @@
                     jnp.where(lane_out == THICK, turn(load, near + HALVES // 8 - THICK), 0.0),
                 )
 
-            total = jnp.zeros((8, LANES), jnp.float32)
             for slot in range(t + 1, SLOTS - 1 - t):
-                acc = advance_slot(src, old, dst, t, slot, *scratch, stiff, pushed(slot), rows)
-                cell = slot - STEPS
-                if 0 <= cell < HALVES:
-                    total = jnp.where((lane8 == cell) | (lane8 == THICK + cell), turn(acc[:8], -cell), total)
-            moved[t] = total * (1.0 / H2)
-            move_copy(t).start()
+                advance_slot(src, old, dst, t, slot, *scratch, stiff, pushed(slot), rows)
 
         from_planes(d4, fields_ref.at[0], range(own_tiles))
         for t in range(STEPS):
             floor_ref[0, t] = dense(arrived[t, 0:8], 1)
-            move_copy(t).wait_send()
+        crown_up().wait_send()
 
     for dx, dy in DIRS:
         @pl.when(exists(dx, dy))
@@ -513,6 +640,10 @@
             @pl.when(wet)
             def _():
                 deep_copy(dx, dy).wait_send()
+
+            @pl.when(jnp.logical_not(wet))
+            def _():
+                crown_copy(dx, dy).wait_send()
 
 
 def deliver(fields_ref, floor_ref, fields_out, floor_out, sem):
@@ -557,8 +688,9 @@
             pltpu.VMEM((STEPS, ROWS, LANES), jnp.float32),
             pltpu.VMEM((STEPS, ROWS, LANES), jnp.float32),
             pltpu.VMEM((STEPS, ROWS, (groups + 2) * LANES), jnp.float32),
-            pltpu.VMEM((STEPS, 8, LANES), jnp.float32),
-            pltpu.VMEM((STEPS, 8, LANES), jnp.float32),
+            pltpu.VMEM((3, ROWS, (groups + 2) * LANES), jnp.float32),
+            pltpu.VMEM((STEPS, ROWS, (groups + 2) * LANES), jnp.float32),
+            *[pltpu.VMEM((3, ROWS, (groups + 4) * LANES), jnp.float32)] * 11,
             dma((4,)),
             dma((3 * len(DIRS),)),
             dma((3 * len(DIRS),)),
@@ -566,8 +698,8 @@
             dma((len(DIRS),)),
             dma((STEPS,)),
             dma((STEPS,)),
-            dma((STEPS,)),
-            dma((STEPS,)),
+            dma((len(DIRS) + 1,)),
+            dma((len(DIRS) + 1,)),
         ],
         compiler_params=pltpu.CompilerParams(collective_id=0, has_side_effects=True),
     )(current, previous, material, prior)

time: 20.2 us -> 19.5 us (0.965)
  the two profiles are of different devices: /device:TPU:216 before, /device:TPU:1 now
where the time goes in v5:
time: 19.5 us; the launch traced here: 19.3 us
  Pallas kernels  18.7 us (96%)
  between operations  0.64 us (3%)
    pallas_call x1, Pallas kernels, on_device(): pl.pallas_call(functools.partial(kernel, sizes, own_tiles), out_shape=(pl...  18 us
    pallas_call x1, Pallas kernels, on_device(): pl.pallas_call(deliver, out_shape=tuple((jax.ShapeDtypeStruct(x.shape, x....  0.68 us

profile of v5, /device:TPU:1, one launch (start us, length us, event | category | flops | bytes accessed | tf_op | source)
XLA Modules:
  0.0 19.3 jit_solution(14200136174820130533)
XLA Ops:
  0.6 18.0 %shard_map.59 = (f32[1,8,4608]{2,1,0:T(8,128)S(1)}, f32[1,4,8,32]{3,2,1,0:T(8,128)S(1)}) custom-call(f32[1,8,4608]{2,1,0:T(8,128)} %cur_hbm.1, f32[1,8,4608]{2,1,0:T(8,128)} %prev_hbm.1, f32[1,8,4608]{2,1,0:T(8,128)} %mat_hbm.1, f32[4,8,32]{2,1,0:T(8,128)} %prior_hbm.1), custom_call_target="tpu_custom_call" | custom-call | tf_op jit(solution)/shard_map/pallas_call | solution.py:674
  18.7 0.7 %shard_map.60 = (f32[1,8,4608]{2,1,0:T(8,128)}, f32[1,4,8,32]{3,2,1,0:T(8,128)}) custom-call(f32[1,8,4608]{2,1,0:T(8,128)S(1)} %get-tuple-element.4.fields_ref, f32[1,4,8,32]{3,2,1,0:T(8,128)S(1)} %get-tuple-element.5.floor_ref), custom_call_target="tpu_custom_call" | custom-call | tf_op jit(solution)/shard_map/pallas_call | solution.py:706

commit v6 on v5

--- a/solution.py
+++ b/solution.py
@@ -206,9 +206,8 @@
     return lap_x, lap_z
 
 
-def top_update(src, old, dst, g, at, sz, sx, ex, self_terms, lap, stiff, pushed, rows):
+def top_update(memo, src, old, dst, g, at, sz, sx, ex, self_terms, lap, stiff, pushed, rows):
     lane = lax.broadcasted_iota(jnp.int32, (rows, LANES), 1)
-    memo = Tiles()
 
     def along(name, ref, c, by):
         return flat_shift(memo, (name, c), lambda n: ref[c, 0:rows, at(n)], lane, g, by)
@@ -286,9 +285,11 @@
 
     pl.semaphore_signal(barrier, inc=1, device_id={"half": 1 - half}, device_id_type=MESH)
 
-    def halo_copies(dx, dy):
+    def halo_copies(dx, dy, water):
+        short = 1 if water and dx and dy else 0
         out = []
-        for n, (ref, depth) in enumerate(((cur, STEPS), (prev, STEPS - 1), (mat, STEPS - 1))):
+        for n, (ref, reach) in enumerate(((cur, STEPS), (prev, STEPS - 1), (mat, STEPS - 1))):
+            depth = reach - short
             width = -(-depth * PLANES // LANES)
             if dy == 0:
                 src_lanes = dst_lanes = lanes_of(0, own_tiles)
@@ -309,6 +310,13 @@
             )
         return out
 
+    def for_rim(dx, dy, act):
+        for water in (True, False):
+            @pl.when(wet == water)
+            def _(water=water):
+                for copy in halo_copies(dx, dy, water):
+                    act(copy)
+
     def deep_lanes(dy, landed):
         if dy == 0:
             return pl.ds(LANES, groups * LANES)
@@ -422,14 +430,12 @@
     for dx, dy in order:
         @pl.when(exists(dx, dy))
         def _(dx=dx, dy=dy):
-            for copy in halo_copies(dx, dy):
-                copy.start()
+            for_rim(dx, dy, lambda copy: copy.start())
 
     def await_rim(dx, dy):
         @pl.when(exists(-dx, -dy))
         def _():
-            for copy in halo_copies(dx, dy):
-                copy.wait_recv()
+            for_rim(dx, dy, lambda copy: copy.wait_recv())
 
     levels = (cur, p1, p2, p3)
     olds = (prev, cur, p1, p2)
@@ -536,10 +542,11 @@
                 tself[0, 0:rows, at(g)] = terms[0][0]
                 tself[1, 0:rows, at(g)] = terms[2][1]
             total = None
+            memo = Tiles()
             for g in range(groups) if last else blocks:
                 source = samples[t, 0:rows, pl.ds((g + 1) * LANES, LANES)]
                 acc = top_update(
-                    tops[t], befores[t], tops[t + 1], g, at, tsz, tsx, tex, tself, tlap, tstiff, source, rows
+                    memo, tops[t], befores[t], tops[t + 1], g, at, tsz, tsx, tex, tself, tlap, tstiff, source, rows
                 )
                 if 0 <= g < groups:
                     tile = turn(jnp.where(within == 0, acc[:8], 0.0), -g)
@@ -634,8 +641,7 @@
     for dx, dy in DIRS:
         @pl.when(exists(dx, dy))
         def _(dx=dx, dy=dy):
-            for copy in halo_copies(dx, dy):
-                copy.wait_send()
+            for_rim(dx, dy, lambda copy: copy.wait_send())
 
             @pl.when(wet)
             def _():

time: 19.5 us -> 19.1 us (0.979)
  Pallas kernels: 18.7 us -> 18.3 us
    pallas_call x1, Pallas kernels: 18 us -> 17.6 us  [on_device(): pl.pallas_call(functools.partial(kernel, sizes, own_tiles), out_shape=(pl...]
where the time goes in v6:
time: 19.1 us; the launch traced here: 18.9 us
  Pallas kernels  18.3 us (96%)
  between operations  0.64 us (3%)
    pallas_call x1, Pallas kernels, on_device(): pl.pallas_call(functools.partial(kernel, sizes, own_tiles), out_shape=(pl...  17.6 us
    pallas_call x1, Pallas kernels, on_device(): pl.pallas_call(deliver, out_shape=tuple((jax.ShapeDtypeStruct(x.shape, x....  0.68 us

profile of v6, /device:TPU:1, one launch (start us, length us, event | category | flops | bytes accessed | tf_op | source)
XLA Modules:
  0.0 18.9 jit_solution(11499117546936470161)
XLA Ops:
  0.6 17.6 %shard_map.59 = (f32[1,8,4608]{2,1,0:T(8,128)S(1)}, f32[1,4,8,32]{3,2,1,0:T(8,128)S(1)}) custom-call(f32[1,8,4608]{2,1,0:T(8,128)} %cur_hbm.1, f32[1,8,4608]{2,1,0:T(8,128)} %prev_hbm.1, f32[1,8,4608]{2,1,0:T(8,128)} %mat_hbm.1, f32[4,8,32]{2,1,0:T(8,128)} %prior_hbm.1), custom_call_target="tpu_custom_call" | custom-call | tf_op jit(solution)/shard_map/pallas_call | solution.py:680
  18.3 0.7 %shard_map.60 = (f32[1,8,4608]{2,1,0:T(8,128)}, f32[1,4,8,32]{3,2,1,0:T(8,128)}) custom-call(f32[1,8,4608]{2,1,0:T(8,128)S(1)} %get-tuple-element.4.fields_ref, f32[1,4,8,32]{3,2,1,0:T(8,128)S(1)} %get-tuple-element.5.floor_ref), custom_call_target="tpu_custom_call" | custom-call | tf_op jit(solution)/shard_map/pallas_call | solution.py:712
